TPU v7x, 32 devices: a whole 2x2x4 slice. The times are simulated.
32 devices in a mesh: section: 4 (over y, core), tensor: 8 (over z, x).
Axes of the slice: x: 2, y: 2, z: 4, core: 2. Of those that a mesh axis runs over, the one named last changes fastest.
Arguments:
- saved_inputs: bfloat16 [4, 4, 256, 1024], P('section', None, 'tensor'), may hold values from -6 to 6
- slot_index: int32 [4, 3], P('section'), may hold values from 0 to 3
- example_lengths: int32 [4, 3, 2], P('section'), may hold values from 1 to 192, 256 in all within a row
- first_grads: bfloat16 [4, 256, 1024], P('section', 'tensor'), may hold values from -6 to 6
- loss_grads: bfloat16 [2, 256, 1024], P(None, 'tensor'), may hold values from -6 to 6
- w_in: bfloat16 [4, 1024, 32768], P('section', None, 'tensor'), may hold values from -0.1875 to 0.1875
- w_out: bfloat16 [4, 32768, 1024], P('section', 'tensor'), may hold values from -0.03125 to 0.03125
Outputs:
- grad_in: bfloat16 [4, 1024, 32768], P('section', None, 'tensor')
- grad_out: bfloat16 [4, 32768, 1024], P('section', 'tensor')
- input_grads: bfloat16 [4, 3, 256, 1024], P('section', None, 'tensor')
Inputs may be any that keep to these rules, and one draw needn't show every extreme that they name: `example_lengths`: the 2 lengths of one microbatch sum to 256.
All inputs are finite; a program needn't handle non-finite values.
Results may differ from a plain program's by a relative error of at most 0.0095.
Values may be sent and summed in bfloat16 or wider, within the bound.
A program may use at most 128 MiB of HBM per device.

v0:
```python
import jax
import jax.numpy as jnp
from jax import lax
from jax.sharding import PartitionSpec as P

GAMMA = 0.01
F32 = jnp.float32
BF16 = jnp.bfloat16


def shifted(value, axis, steps):
    count = lax.axis_size(axis)
    first, last = (max(0, -steps), min(count, count - steps))
    return lax.ppermute(value, axis, [(source, source + steps) for source in range(first, last)])


def membership(lengths, tokens):
    ends = jnp.cumsum(lengths)
    position = jnp.arange(tokens, dtype=jnp.int32)
    example_id = jnp.sum((position[:, None] >= ends[None, :-1]).astype(jnp.int32), axis=1)
    labels = jnp.arange(lengths.shape[0], dtype=jnp.int32)
    return (example_id[:, None] == labels[None, :]).astype(F32)


def spread(value, axis):
    copies = jnp.broadcast_to(value[None], (lax.axis_size(axis),) + value.shape)
    return lax.all_to_all(copies, axis, 0, 0)


def gram(value):
    return lax.dot_general(value, value, (((1,), (1,)), ((), ())), preferred_element_type=F32)


def per_device(saved_inputs, slot_index, example_lengths, first_grads, loss_grads, w_in, w_out):
    section_count = lax.axis_size("section")
    parts = lax.axis_size("tensor")
    is_last = lax.axis_index("section") == section_count - 1
    first = w_in[0]
    second = w_out[0]
    slot_count = loss_grads.shape[0] + 1
    rows, width = first_grads.shape[1:]
    hidden_all = first.shape[1] * parts
    picked = [
        lax.dynamic_index_in_dim(saved_inputs[0], slot_index[0, slot], 0, keepdims=False)
        for slot in range(slot_count)
    ]
    tokens = parts * rows
    opening = spread(jnp.concatenate([picked[0], first_grads[0]]), "tensor")
    later = spread(jnp.concatenate(picked[1:]), "tensor")
    every_input = [opening[:, :rows].reshape(tokens, width)]
    for slot in range(slot_count - 1):
        every_input.append(later[:, slot * rows : (slot + 1) * rows].reshape(tokens, width))
    incoming = first_grads[0]
    results, dzs, hiddens, grad_list, members, squares = [], [], [], [], [], []
    for slot in range(slot_count):
        inputs = every_input[slot]
        if slot == 0:
            grads = opening[:, rows:].reshape(tokens, width)
        else:
            grads = spread(incoming, "tensor").reshape(tokens, width)
        z = jnp.dot(inputs, first, preferred_element_type=F32)
        relu = jnp.maximum(z, 0.0)
        hidden = (relu * relu).astype(BF16)
        back = jnp.einsum("td,fd->tf", grads, second, preferred_element_type=F32)
        dz = (2.0 * relu * back).astype(BF16)
        own_terms = jnp.einsum("tf,df->td", dz, first, preferred_element_type=F32).astype(BF16)
        pieces = lax.all_to_all(own_terms.reshape(parts, rows, width), "tensor", 0, 0)
        shares = jnp.sum(pieces.astype(F32), axis=0)
        passing = (incoming.astype(F32) + shares).astype(BF16)
        results.append(passing)
        if slot + 1 < slot_count:
            arrived = shifted(passing, "section", -1)
            incoming = jnp.where(is_last, loss_grads[slot], arrived)
        member = membership(example_lengths[0, slot], inputs.shape[0])
        paired = gram(inputs) * gram(dz) + gram(hidden) * gram(grads)
        per_row = jnp.stack([jnp.sum(paired * member[:, e][None, :], axis=1) for e in range(member.shape[1])], axis=1)
        squares.append(jnp.sum(member * per_row, axis=0))
        dzs.append(dz)
        hiddens.append(hidden)
        grad_list.append(grads)
        members.append(member)
    local = jnp.stack(squares)
    total = jnp.sum(spread(local, "tensor"), axis=0)
    factor = 1.0 / (jnp.sqrt(total / (width * hidden_all)) + GAMMA)
    token_factor = jnp.concatenate([jnp.sum(m * factor[i][None, :], axis=1) for i, m in enumerate(members)])[:, None]
    xc = (jnp.concatenate(every_input).astype(F32) * token_factor).astype(BF16)
    dyc = (jnp.concatenate(grad_list).astype(F32) * token_factor).astype(BF16)
    grad_in = jnp.einsum("td,tf->df", xc, jnp.concatenate(dzs), preferred_element_type=F32).astype(BF16)[None]
    grad_out = jnp.einsum("tf,td->fd", jnp.concatenate(hiddens), dyc, preferred_element_type=F32).astype(BF16)[None]
    input_grads = jnp.stack(results)[None]
    return (grad_in, grad_out, input_grads)


def solution(mesh):
    return jax.shard_map(
        per_device,
        mesh=mesh,
        in_specs=(
            P("section", None, "tensor", None),
            P("section", None),
            P("section", None, None),
            P("section", "tensor", None),
            P(None, "tensor", None),
            P("section", None, "tensor"),
            P("section", "tensor", None),
        ),
        out_specs=(
            P("section", None, "tensor"),
            P("section", "tensor", None),
            P("section", None, "tensor", None),
        ),
        check_vma=False,
    )
```

profile of v0, /device:TPU:0, one launch (start us, length us, event | category | flops | bytes accessed | tf_op | source)
XLA Modules:
  0.0 227.8 jit_solution(14259533319539249769)
XLA Ops:
  10.7 7.3 %all-to-all-start = ((bf16[8,64,1024]{2,1,0:T(8,128)(2,1)}), bf16[8,64,1024]{2,1,0:T(8,128)(2,1)S(1)}, u32[]{:S(2)}, u32[]{:S(2)}) async-start(bf16[8,64,1024]{2,1,0:T(8,128)(2,1)} %broadcast_in_dim.16), calls=%async_computation | async-start | bytes 2097152 | tf_op jit(solution)/shard_map/all_to_all | solution.py:27
  20.6 23.1 %all-to-all-done = bf16[8,64,1024]{2,1,0:T(8,128)(2,1)S(1)} async-done(((bf16[8,64,1024]{2,1,0:T(8,128)(2,1)}), bf16[8,64,1024]{2,1,0:T(8,128)(2,1)S(1)}, u32[]{:S(2)}, u32[]{:S(2)}) %all-to-all-start) | async-done | bytes 1048608 | tf_op jit(solution)/shard_map/all_to_all | solution.py:27
  44.9 4.2 %all-to-all-start.1 = ((bf16[8,64,1024]{2,1,0:T(8,128)(2,1)}), bf16[8,64,1024]{2,1,0:T(8,128)(2,1)}, u32[]{:S(2)}, u32[]{:S(2)}) async-start(bf16[8,64,1024]{2,1,0:T(8,128)(2,1)} %broadcast_in_dim.17), calls=%async_computation.1 | async-start | bytes 2097152 | tf_op jit(solution)/shard_map/all_to_all | solution.py:27
  49.3 8.9 %multiply_convert_fusion.2 = (bf16[256,4096]{1,0:T(8,128)(2,1)}, f32[256,4096]{1,0:T(8,128)}) fusion(bf16[256,1024]{1,0:T(8,128)(2,1)S(1)} %bitcast.150, bf16[1,1024,4096]{2,1,0:T(8,128)(2,1)} %param.12), kind=kOutput, calls=%fused_computation.41 | convolution fusion | flops 2150629376 | bytes 15204352 | tf_op jit(solution)/shard_map/dot_general | solution.py:61
  58.2 4.8 %fusion.52 = bf16[256,4096]{1,0:T(8,128)(2,1)S(1)} fusion(bf16[256,1024]{1,0:T(8,128)(2,1)S(1)} %bitcast.153, bf16[1,4096,1024]{2,1,0:T(8,128)(2,1)S(1)} %bitcast.186, f32[256,4096]{1,0:T(8,128)} %get-tuple-element.36), kind=kOutput, calls=%fused_computation.38 | convolution fusion | flops 2150629376 | bytes 15204352 | tf_op jit(solution)/shard_map/td,fd->tf/dot_general | solution.py:64
  66.2 8.5 %all-to-all-done.1 = bf16[8,64,1024]{2,1,0:T(8,128)(2,1)} async-done(((bf16[8,64,1024]{2,1,0:T(8,128)(2,1)}), bf16[8,64,1024]{2,1,0:T(8,128)(2,1)}, u32[]{:S(2)}, u32[]{:S(2)}) %all-to-all-start.1) | async-done | bytes 1048608 | tf_op jit(solution)/shard_map/all_to_all | solution.py:27
  74.7 4.1 %all-to-all-start.2 = ((bf16[8,32,1024]{2,1,0:T(8,128)(2,1)}), bf16[8,32,1024]{2,1,0:T(8,128)(2,1)}, u32[]{:S(2)}, u32[]{:S(2)}) async-start(bf16[8,32,1024]{2,1,0:T(8,128)(2,1)} %bitcast.164), calls=%async_computation.2 | async-start | bytes 1048576 | tf_op jit(solution)/shard_map/all_to_all | solution.py:67
  85.8 7.2 %all-to-all-done.2 = bf16[8,32,1024]{2,1,0:T(8,128)(2,1)} async-done(((bf16[8,32,1024]{2,1,0:T(8,128)(2,1)}), bf16[8,32,1024]{2,1,0:T(8,128)(2,1)}, u32[]{:S(2)}, u32[]{:S(2)}) %all-to-all-start.2) | async-done | bytes 524320 | tf_op jit(solution)/shard_map/all_to_all | solution.py:67
  100.5 3.7 %all-to-all-start.3 = ((bf16[8,32,1024]{2,1,0:T(8,128)(2,1)}), bf16[8,32,1024]{2,1,0:T(8,128)(2,1)S(1)}, u32[]{:S(2)}, u32[]{:S(2)}) async-start(bf16[8,32,1024]{2,1,0:T(8,128)(2,1)} %broadcast_in_dim.18), calls=%async_computation.3 | async-start | bytes 1048576 | tf_op jit(solution)/shard_map/all_to_all | solution.py:27
  104.2 8.0 %multiply_convert_fusion.1 = (bf16[256,4096]{1,0:T(8,128)(2,1)S(1)}, f32[256,4096]{1,0:T(8,128)}) fusion(bf16[256,1024]{1,0:T(8,128)(2,1)} %bitcast.159, bf16[1,1024,4096]{2,1,0:T(8,128)(2,1)} %param.12), kind=kOutput, calls=%fused_computation.40 | convolution fusion | flops 2150629376 | bytes 15204352 | tf_op jit(solution)/shard_map/dot_general | solution.py:61
  114.9 3.9 %all-to-all-done.3 = bf16[8,32,1024]{2,1,0:T(8,128)(2,1)S(1)} async-done(((bf16[8,32,1024]{2,1,0:T(8,128)(2,1)}), bf16[8,32,1024]{2,1,0:T(8,128)(2,1)S(1)}, u32[]{:S(2)}, u32[]{:S(2)}) %all-to-all-start.3) | async-done | bytes 524320 | tf_op jit(solution)/shard_map/all_to_all | solution.py:27
  118.8 6.9 %fusion.49 = bf16[256,4096]{1,0:T(8,128)(2,1)S(1)} fusion(bf16[256,1024]{1,0:T(8,128)(2,1)S(1)} %bitcast.144, bf16[1,4096,1024]{2,1,0:T(8,128)(2,1)} %param.13, f32[256,4096]{1,0:T(8,128)} %get-tuple-element.34), kind=kOutput, calls=%fused_computation.37 | convolution fusion | flops 2150629376 | bytes 15204352 | tf_op jit(solution)/shard_map/td,fd->tf/dot_general | solution.py:64
  125.8 7.3 %fusion.70 = bf16[256,1024]{1,0:T(8,128)(2,1)} fusion(bf16[256,4096]{1,0:T(8,128)(2,1)S(1)} %fusion.49, bf16[1,1024,4096]{2,1,0:T(8,128)(2,1)} %param.12), kind=kOutput, calls=%fused_computation.57 | convolution fusion | flops 2147745792 | bytes 11010048 | tf_op jit(solution)/shard_map/tf,df->td/dot_general | solution.py:66
  133.1 4.7 %all-to-all-start.4 = ((bf16[8,32,1024]{2,1,0:T(8,128)(2,1)}), bf16[8,32,1024]{2,1,0:T(8,128)(2,1)}, u32[]{:S(2)}, u32[]{:S(2)}) async-start(bf16[8,32,1024]{2,1,0:T(8,128)(2,1)} %bitcast.165), calls=%async_computation.4 | async-start | bytes 1048576 | tf_op jit(solution)/shard_map/all_to_all | solution.py:67
  137.8 7.8 %multiply_convert_fusion = (bf16[256,4096]{1,0:T(8,128)(2,1)S(1)}, f32[256,4096]{1,0:T(8,128)}) fusion(bf16[256,1024]{1,0:T(8,128)(2,1)S(1)} %bitcast.156, bf16[1,1024,4096]{2,1,0:T(8,128)(2,1)} %param.12), kind=kOutput, calls=%fused_computation.39 | convolution fusion | flops 2150629376 | bytes 15204352 | tf_op jit(solution)/shard_map/dot_general | solution.py:61
  147.7 5.5 %all-to-all-done.4 = bf16[8,32,1024]{2,1,0:T(8,128)(2,1)} async-done(((bf16[8,32,1024]{2,1,0:T(8,128)(2,1)}), bf16[8,32,1024]{2,1,0:T(8,128)(2,1)}, u32[]{:S(2)}, u32[]{:S(2)}) %all-to-all-start.4) | async-done | bytes 524320 | tf_op jit(solution)/shard_map/all_to_all | solution.py:67
  158.4 3.7 %all-to-all-start.5 = ((bf16[8,32,1024]{2,1,0:T(8,128)(2,1)}), bf16[8,32,1024]{2,1,0:T(8,128)(2,1)S(1)}, u32[]{:S(2)}, u32[]{:S(2)}) async-start(bf16[8,32,1024]{2,1,0:T(8,128)(2,1)} %broadcast_in_dim.19), calls=%async_computation.5 | async-start | bytes 1048576 | tf_op jit(solution)/shard_map/all_to_all | solution.py:27
  167.6 9.1 %all-to-all-done.5 = bf16[8,32,1024]{2,1,0:T(8,128)(2,1)S(1)} async-done(((bf16[8,32,1024]{2,1,0:T(8,128)(2,1)}), bf16[8,32,1024]{2,1,0:T(8,128)(2,1)S(1)}, u32[]{:S(2)}, u32[]{:S(2)}) %all-to-all-start.5) | async-done | bytes 524320 | tf_op jit(solution)/shard_map/all_to_all | solution.py:27
  176.7 6.9 %fusion.46 = bf16[256,4096]{1,0:T(8,128)(2,1)S(1)} fusion(bf16[256,1024]{1,0:T(8,128)(2,1)S(1)} %bitcast.147, bf16[1,4096,1024]{2,1,0:T(8,128)(2,1)} %param.13, f32[256,4096]{1,0:T(8,128)} %get-tuple-element.32), kind=kOutput, calls=%fused_computation.36 | convolution fusion | flops 2150629376 | bytes 15204352 | tf_op jit(solution)/shard_map/td,fd->tf/dot_general | solution.py:64
  186.7 4.8 %all-to-all-start.6 = ((f32[8,3,2]{1,2,0:T(2,128)}), f32[8,3,2]{1,2,0:T(2,128)S(1)}, u32[]{:S(2)}, u32[]{:S(2)}) async-start(f32[8,3,2]{1,2,0:T(2,128)} %broadcast_in_dim.20), calls=%async_computation.6 | async-start | bytes 16384 | tf_op jit(solution)/shard_map/all_to_all | solution.py:27
  191.4 7.2 %fusion.73 = bf16[256,1024]{1,0:T(8,128)(2,1)} fusion(bf16[256,4096]{1,0:T(8,128)(2,1)} %copy-done.4, bf16[1,1024,4096]{2,1,0:T(8,128)(2,1)} %param.12), kind=kOutput, calls=%fused_computation.58 | convolution fusion | flops 2147745792 | bytes 11010048 | tf_op jit(solution)/shard_map/tf,df->td/dot_general | solution.py:66
  198.6 6.0 %all-to-all-start.7 = ((bf16[8,32,1024]{2,1,0:T(8,128)(2,1)}), bf16[8,32,1024]{2,1,0:T(8,128)(2,1)}, u32[]{:S(2)}, u32[]{:S(2)}) async-start(bf16[8,32,1024]{2,1,0:T(8,128)(2,1)} %bitcast.163), calls=%async_computation.7 | async-start | bytes 1048576 | tf_op jit(solution)/shard_map/all_to_all | solution.py:67
  205.1 11.3 %convert_bitcast_fusion = bf16[1,4096,1024]{2,1,0:T(8,128)(2,1)} fusion(bf16[256,4096]{1,0:T(8,128)(2,1)} %copy-done.3, bf16[256,4096]{1,0:T(8,128)(2,1)} %copy-done, bf16[256,4096]{1,0:T(8,128)(2,1)} %get-tuple-element.35, bf16[256,1024]{1,0:T(8,128)(2,1)S(1)} %bitcast.149, bf16[256,1024]{1,0:T(8,128)(2,1)S(1)} %bitcast.146, ...), kind=kOutput, calls=%fused_computation.18 | convolution fusion | flops 6471811072 | bytes 16256000 | tf_op jit(solution)/shard_map/tf,td->fd/dot_general | solution.py:89
  216.5 9.4 %convert_bitcast_fusion.1 = bf16[1,1024,4096]{2,1,0:T(8,128)(2,1)} fusion(bf16[256,4096]{1,0:T(8,128)(2,1)S(1)} %copy-done.5, bf16[256,4096]{1,0:T(8,128)(2,1)S(1)} %copy-done.2, bf16[256,4096]{1,0:T(8,128)(2,1)S(1)} %fusion.52, bf16[256,1024]{1,0:T(8,128)(2,1)S(1)} %bitcast.158, bf16[256,1024]{1,0:T(8,128)(2,1)S(1)} %bitcast.161, ...), kind=kOutput, calls=%fused_computation.19 | convolution fusion | flops 6471811072 | bytes 16256000 | tf_op jit(solution)/shard_map/td,tf->df/dot_general | solution.py:88
  (134 shorter events, 46.2 us)
Async XLA Ops:
  0.6 17.4 %copy-start.23 = (s32[1,3,2]{1,2,0:T(2,128)S(1)}, s32[1,3,2]{1,2,0:T(2,128)}, u32[]{:S(2)}) copy-start(s32[1,3,2]{1,2,0:T(2,128)} %param.9) | copy-start | bytes 76
  10.7 33.0 %all-to-all-start = ((bf16[8,64,1024]{2,1,0:T(8,128)(2,1)}), bf16[8,64,1024]{2,1,0:T(8,128)(2,1)S(1)}, u32[]{:S(2)}, u32[]{:S(2)}) async-start(bf16[8,64,1024]{2,1,0:T(8,128)(2,1)} %broadcast_in_dim.16), calls=%async_computation | async-start | bytes 2097152 | tf_op jit(solution)/shard_map/all_to_all | solution.py:27
  44.9 29.8 %all-to-all-start.1 = ((bf16[8,64,1024]{2,1,0:T(8,128)(2,1)}), bf16[8,64,1024]{2,1,0:T(8,128)(2,1)}, u32[]{:S(2)}, u32[]{:S(2)}) async-start(bf16[8,64,1024]{2,1,0:T(8,128)(2,1)} %broadcast_in_dim.17), calls=%async_computation.1 | async-start | bytes 2097152 | tf_op jit(solution)/shard_map/all_to_all | solution.py:27
  49.3 32.6 %copy-start.8 = (bf16[8,32,1024]{2,1,0:T(8,128)(2,1)}, bf16[8,32,1024]{2,1,0:T(8,128)(2,1)S(1)}, u32[]{:S(2)}) copy-start(bf16[8,32,1024]{2,1,0:T(8,128)(2,1)S(1)} %get-tuple-element.18) | copy-start | bytes 1572868
  49.3 47.0 %copy-start.6 = (bf16[8,32,1024]{2,1,0:T(8,128)(2,1)}, bf16[8,32,1024]{2,1,0:T(8,128)(2,1)S(1)}, u32[]{:S(2)}) copy-start(bf16[8,32,1024]{2,1,0:T(8,128)(2,1)S(1)} %get-tuple-element.17) | copy-start | bytes 1572868
  49.3 13.8 %slice-start.2 = ((s8[8388608]{0:T(1024)(128)(4,1)}), s8[4194304]{0:T(1024)(128)(4,1)S(1)}, s32[]{:S(2)}) async-start(s8[8388608]{0:T(1024)(128)(4,1)} %bitcast.187), calls=%async_computation.10 | async-start | bytes 8388608
  74.7 18.2 %all-to-all-start.2 = ((bf16[8,32,1024]{2,1,0:T(8,128)(2,1)}), bf16[8,32,1024]{2,1,0:T(8,128)(2,1)}, u32[]{:S(2)}, u32[]{:S(2)}) async-start(bf16[8,32,1024]{2,1,0:T(8,128)(2,1)} %bitcast.164), calls=%async_computation.2 | async-start | bytes 1048576 | tf_op jit(solution)/shard_map/all_to_all | solution.py:67
  85.1 52.8 %copy-start.9 = (bf16[8,32,1024]{2,1,0:T(8,128)(2,1)}, bf16[8,32,1024]{2,1,0:T(8,128)(2,1)S(1)}, u32[]{:S(2)}) copy-start(bf16[8,32,1024]{2,1,0:T(8,128)(2,1)S(1)} %get-tuple-element.15) | copy-start | bytes 1572868
  94.9 3.2 %collective-permute-start = (bf16[32,1024]{1,0:T(8,128)(2,1)S(1)}, bf16[32,1024]{1,0:T(8,128)(2,1)S(1)}, u32[]{:S(2)}, u32[]{:S(2)}) collective-permute-start(bf16[32,1024]{1,0:T(8,128)(2,1)S(1)} %add_convert_fusion.2), channel_id=1, source_target_pairs={{8,0},{16,8},{24,16},{9,1},{17,9},{25,17},{10,2},{18,10},{26,18},{... | collective-permute-start | bytes 196616 | tf_op jit(solution)/shard_map/ppermute | solution.py:14
  100.5 18.4 %all-to-all-start.3 = ((bf16[8,32,1024]{2,1,0:T(8,128)(2,1)}), bf16[8,32,1024]{2,1,0:T(8,128)(2,1)S(1)}, u32[]{:S(2)}, u32[]{:S(2)}) async-start(bf16[8,32,1024]{2,1,0:T(8,128)(2,1)} %broadcast_in_dim.18), calls=%async_computation.3 | async-start | bytes 1048576 | tf_op jit(solution)/shard_map/all_to_all | solution.py:27
  133.1 20.1 %all-to-all-start.4 = ((bf16[8,32,1024]{2,1,0:T(8,128)(2,1)}), bf16[8,32,1024]{2,1,0:T(8,128)(2,1)}, u32[]{:S(2)}, u32[]{:S(2)}) async-start(bf16[8,32,1024]{2,1,0:T(8,128)(2,1)} %bitcast.165), calls=%async_computation.4 | async-start | bytes 1048576 | tf_op jit(solution)/shard_map/all_to_all | solution.py:67
  145.6 11.9 %copy-start.22 = (bf16[2,32,1024]{2,1,0:T(8,128)(2,1)S(1)}, bf16[2,32,1024]{2,1,0:T(8,128)(2,1)}, u32[]{:S(2)}) copy-start(bf16[2,32,1024]{2,1,0:T(8,128)(2,1)} %param.11) | copy-start | bytes 393220
  154.4 3.1 %collective-permute-start.1 = (bf16[32,1024]{1,0:T(8,128)(2,1)S(1)}, bf16[32,1024]{1,0:T(8,128)(2,1)S(1)}, u32[]{:S(2)}, u32[]{:S(2)}) collective-permute-start(bf16[32,1024]{1,0:T(8,128)(2,1)S(1)} %add_convert_fusion.1), channel_id=1, source_target_pairs={{8,0},{16,8},{24,16},{9,1},{17,9},{25,17},{10,2},{18,10},{26,18},{... | collective-permute-start | bytes 196616 | tf_op jit(solution)/shard_map/ppermute | solution.py:14
  158.4 18.3 %all-to-all-start.5 = ((bf16[8,32,1024]{2,1,0:T(8,128)(2,1)}), bf16[8,32,1024]{2,1,0:T(8,128)(2,1)S(1)}, u32[]{:S(2)}, u32[]{:S(2)}) async-start(bf16[8,32,1024]{2,1,0:T(8,128)(2,1)} %broadcast_in_dim.19), calls=%async_computation.5 | async-start | bytes 1048576 | tf_op jit(solution)/shard_map/all_to_all | solution.py:27
  186.7 12.0 %all-to-all-start.6 = ((f32[8,3,2]{1,2,0:T(2,128)}), f32[8,3,2]{1,2,0:T(2,128)S(1)}, u32[]{:S(2)}, u32[]{:S(2)}) async-start(f32[8,3,2]{1,2,0:T(2,128)} %broadcast_in_dim.20), calls=%async_computation.6 | async-start | bytes 16384 | tf_op jit(solution)/shard_map/all_to_all | solution.py:27
  198.6 27.3 %all-to-all-start.7 = ((bf16[8,32,1024]{2,1,0:T(8,128)(2,1)}), bf16[8,32,1024]{2,1,0:T(8,128)(2,1)}, u32[]{:S(2)}, u32[]{:S(2)}) async-start(bf16[8,32,1024]{2,1,0:T(8,128)(2,1)} %bitcast.163), calls=%async_computation.7 | async-start | bytes 1048576 | tf_op jit(solution)/shard_map/all_to_all | solution.py:67
  205.0 11.4 %copy-start.2 = (bf16[256,4096]{1,0:T(8,128)(2,1)S(1)}, bf16[256,4096]{1,0:T(8,128)(2,1)}, u32[]{:S(2)}) copy-start(bf16[256,4096]{1,0:T(8,128)(2,1)} %copy-done.1) | copy-start | bytes 6291460
  205.1 11.4 %copy-start.5 = (bf16[256,4096]{1,0:T(8,128)(2,1)S(1)}, bf16[256,4096]{1,0:T(8,128)(2,1)}, u32[]{:S(2)}) copy-start(bf16[256,4096]{1,0:T(8,128)(2,1)} %copy-done.4) | copy-start | bytes 6291460
  205.1 11.4 %copy-start.7 = (bf16[8,32,1024]{2,1,0:T(8,128)(2,1)S(1)}, bf16[8,32,1024]{2,1,0:T(8,128)(2,1)}, u32[]{:S(2)}) copy-start(bf16[8,32,1024]{2,1,0:T(8,128)(2,1)} %copy-done.6) | copy-start | bytes 1572868
  205.1 11.4 %copy-start.11 = (bf16[8,32,1024]{2,1,0:T(8,128)(2,1)S(1)}, bf16[8,32,1024]{2,1,0:T(8,128)(2,1)}, u32[]{:S(2)}) copy-start(bf16[8,32,1024]{2,1,0:T(8,128)(2,1)} %copy-done.9) | copy-start | bytes 1572868
  205.1 11.4 %copy-start.13 = (bf16[8,32,1024]{2,1,0:T(8,128)(2,1)S(1)}, bf16[8,32,1024]{2,1,0:T(8,128)(2,1)}, u32[]{:S(2)}) copy-start(bf16[8,32,1024]{2,1,0:T(8,128)(2,1)} %get-tuple-element.16) | copy-start | bytes 1572868
  216.5 10.6 %copy-start.16 = (bf16[32,1024]{1,0:T(8,128)(2,1)S(1)}, bf16[32,1024]{1,0:T(8,128)(2,1)}, u32[]{:S(2)}) copy-start(bf16[32,1024]{1,0:T(8,128)(2,1)} %copy-done.15) | copy-start | bytes 196612
  216.5 10.6 %copy-start.20 = (bf16[32,1024]{1,0:T(8,128)(2,1)S(1)}, bf16[32,1024]{1,0:T(8,128)(2,1)}, u32[]{:S(2)}) copy-start(bf16[32,1024]{1,0:T(8,128)(2,1)} %copy-done.19) | copy-start | bytes 196612
  216.5 10.6 %copy-start.21 = (bf16[1,32,1024]{2,1,0:T(8,128)(2,1)S(1)}, bf16[1,32,1024]{2,1,0:T(8,128)(2,1)}, u32[]{:S(2)}) copy-start(bf16[1,32,1024]{2,1,0:T(8,128)(2,1)} %fusion.79) | copy-start | bytes 196612
  (20 other events, 85.8 us)
where the time goes:
time: 229 us; the launch traced here: 228 us
  matrix products  95.6 us (42%)
  waiting for transfers between devices  58.5 us (26%)
  starting transfers between devices  41.1 us (18%)
  local copies, waits for them, and re-layouts  15.4 us (7%)
  other arithmetic  10.1 us (4%)
  between operations  7.11 us (3%)
    all_to_all x5, waiting for transfers between devices, spread(): return lax.all_to_all(copies, axis, 0, 0)  44.7 us
    dot_general x3, matrix products, per_device(): z = jnp.dot(inputs, first, preferred_element_type=F32)  24.7 us
    all_to_all x5, starting transfers between devices, spread(): return lax.all_to_all(copies, axis, 0, 0)  23.7 us
    dot_general x3, matrix products, per_device(): back = jnp.einsum('td,fd->tf', grads, second, preferred_element_type=F32)  18.7 us
    dot_general x3, matrix products, per_device(): jnp.einsum('tf,df->td', dz, first, preferred_element_type=F32).astype(BF16)  17.7 us
    all_to_all x3, starting transfers between devices, per_device(): lax.all_to_all(own_terms.reshape(parts, rows, width), 'tensor', 0, 0)  14.9 us
    dot_general x12, matrix products, gram(): lax.dot_general(value, value, (((1,), (1,)), ((), ())), preferred_element...  13.9 us
    all_to_all x3, waiting for transfers between devices, per_device(): lax.all_to_all(own_terms.reshape(parts, rows, width), 'tensor', 0, 0)  12.7 us
  transfers between devices with their start and end apart: 10, of which 7 were waited for; matrix products, arithmetic and copies ran while one was open for 35% of the time, Pallas kernels for 0%

commit v1 on v0

--- a/solution.py
+++ b/solution.py
@@ -1,11 +1,462 @@
+import functools
+
 import jax
 import jax.numpy as jnp
 from jax import lax
+from jax.experimental import pallas as pl
+from jax.experimental.pallas import tpu as pltpu
 from jax.sharding import PartitionSpec as P
 
 GAMMA = 0.01
 F32 = jnp.float32
 BF16 = jnp.bfloat16
+MESH = pl.DeviceIdType.MESH
+NT = (((1,), (1,)), ((), ()))
+TN = (((0,), (0,)), ((), ()))
+
+
+def dot(a, b, dims):
+    return lax.dot_general(a, b, dims, preferred_element_type=F32)
+
+
+def chain_kernel(
+    cfg,
+    index_ref, lengths_ref, saved_ref, first_ref, loss_ref, win_hbm, wout_hbm,
+    xct_hbm, dyc_hbm, h_hbm, dz_hbm, res_hbm,
+    win, wout, xg, dyb, h, dz, rbuf, acc, own, rxs, rxr, rzs, rzr, res, sqs, sqr, xct, dyc,
+    w_sem, ag_send, ag_recv, fw_send, fw_recv, rx_send, rx_recv, rz_send, rz_recv,
+    sh_send, sh_recv, af_send, af_recv, sq_send, sq_recv, out_sem,
+):
+    sections, parts, nz, slots, rows, width, local, chunks, examples, hidden_all = cfg
+    cols = width // chunks
+    tokens = parts * rows
+    tile = min(512, local)
+    tiles = local // tile
+    s = lax.axis_index("section")
+    p = lax.axis_index("tensor")
+    z = p // 2
+    x = p % 2
+    is_last = s == sections - 1
+    partner = {"section": s, "tensor": z * 2 + (1 - x)}
+
+    def zpeer(j):
+        return {"section": s, "tensor": ((z + j) % nz) * 2 + x}
+
+    def behind(j):
+        return {"section": s - 1, "tensor": ((z + j) % nz) * 2 + x}
+
+    pieces = 4
+    span_in, span_out = local // pieces, local // pieces
+    for k in range(pieces):
+        pltpu.make_async_copy(win_hbm.at[0, :, pl.ds(k * span_in, span_in)], win.at[:, pl.ds(k * span_in, span_in)], w_sem.at[0, k]).start()
+    for k in range(pieces):
+        pltpu.make_async_copy(wout_hbm.at[0, pl.ds(k * span_out, span_out)], wout.at[pl.ds(k * span_out, span_out)], w_sem.at[1, k]).start()
+
+    for t in range(slots):
+        xg[t, z, x] = saved_ref[0, index_ref[0, t]]
+    for c in range(chunks):
+        dyb[0, c, z, x] = first_ref[0, :, pl.ds(c * cols, cols)]
+
+    @pl.when(is_last)
+    def _():
+        for t in range(1, slots):
+            for c in range(chunks):
+                dyb[t, c, z, x] = loss_ref[t - 1, :, pl.ds(c * cols, cols)]
+
+    barrier = pltpu.get_barrier_semaphore()
+    for j in range(1, parts):
+        pl.semaphore_signal(barrier, inc=1, device_id={"section": s, "tensor": (p + j) % parts}, device_id_type=MESH)
+
+    for side in (1, sections - 1):
+        for j in range(nz):
+            pl.semaphore_signal(barrier, inc=1, device_id={"section": (s + side) % sections, "tensor": ((z + j) % nz) * 2 + x}, device_id_type=MESH)
+    pl.semaphore_wait(barrier, parts - 1 + 2 * nz)
+
+    def block(k, source):
+        if k < slots:
+            return xg.at[k, source, x]
+        return dyb.at[k - slots, :, source, x]
+
+    def ag_copy(k, j, to_partner):
+        if to_partner:
+            ref = block(k, (z + nz - j) % nz)
+            return pltpu.make_async_remote_copy(ref, ref, fw_send.at[k, j], fw_recv.at[k, j], device_id=partner, device_id_type=MESH)
+        ref = block(k, z)
+        return pltpu.make_async_remote_copy(ref, ref, ag_send.at[k, j], ag_recv.at[k, j], device_id=zpeer(j), device_id_type=MESH)
+
+    def ag_open(k):
+        for j in range(1, nz):
+            ag_copy(k, j, False).start()
+
+    def ag_forward(k):
+        ag_copy(k, 0, True).start()
+        for j in range(1, nz):
+            ag_copy(k, j, False).wait_recv()
+            ag_copy(k, j, True).start()
+
+    def ag_finish(k):
+        for j in range(nz):
+            ag_copy(k, j, True).wait_recv()
+
+    def ag_drain(k):
+        for j in range(nz):
+            if j:
+                ag_copy(k, j, False).wait_send()
+            ag_copy(k, j, True).wait_send()
+
+    def z_tiles(t, lo, hi):
+        def body(i, carry):
+            at = pl.ds(pl.multiple_of(i * tile, tile), tile)
+            zz = jnp.dot(xg[t].reshape(tokens, width), win[:, at], preferred_element_type=F32)
+            r = jnp.maximum(zz, 0.0)
+            rbuf[:, at] = r
+            h[t, :, at] = (r * r).astype(BF16)
+            return carry
+
+        lax.fori_loop(lo, hi, body, 0)
+
+    def back_all(t):
+        def body(i, carry):
+            at = pl.ds(pl.multiple_of(i * tile, tile), tile)
+            grads = jnp.concatenate([dyb[t, c].reshape(tokens, cols) for c in range(chunks)], axis=1)
+            dh = dot(grads, wout[at, :], NT)
+            dz[t, :, at] = (2.0 * rbuf[:, at] * dh).astype(BF16)
+            return carry
+
+        lax.fori_loop(0, tiles, body, 0)
+
+    def back_chunk(t, c, mode):
+        def body(i, carry):
+            at = pl.ds(pl.multiple_of(i * tile, tile), tile)
+            dh = dot(dyb[t, c].reshape(tokens, cols), wout[at, c * cols:(c + 1) * cols], NT)
+            if mode > 0:
+                dh = dh + acc[:, at]
+            if mode < 2:
+                acc[:, at] = dh
+            else:
+                dz[t, :, at] = (2.0 * rbuf[:, at] * dh).astype(BF16)
+            return carry
+
+        lax.fori_loop(0, tiles, body, 0)
+
+    def rx_copy(t, c):
+        return pltpu.make_async_remote_copy(rxs.at[t, c], rxr.at[t, c], rx_send.at[t, c], rx_recv.at[t, c], device_id=partner, device_id_type=MESH)
+
+    def rz_copy(t, c, j):
+        return pltpu.make_async_remote_copy(rzs.at[t, c, (z + j) % nz], rzr.at[t, c, j], rz_send.at[t, c, j], rz_recv.at[t, c, j], device_id=zpeer(j), device_id_type=MESH)
+
+    def sh_copy(t, c, j):
+        return pltpu.make_async_remote_copy(res.at[t, c], dyb.at[t + 1, c, z, x], sh_send.at[t, c, j], sh_recv.at[t, c, j], device_id=behind(j), device_id_type=MESH)
+
+    def af_copy(t, c):
+        ref = dyb.at[t + 1, c, :, x]
+        return pltpu.make_async_remote_copy(ref, ref, af_send.at[t, c], af_recv.at[t, c], device_id=partner, device_id_type=MESH)
+
+    def over_chunks(body):
+        def step(c, carry):
+            body(c)
+            return carry
+
+        lax.fori_loop(0, chunks, step, 0)
+
+    def partial_dx(t):
+        def body(c):
+            wide = win[pl.ds(pl.multiple_of(c * cols, cols), cols), :]
+            part = dot(dz[t], wide, NT).reshape(nz, 2, rows, cols)
+            first_half, second_half = part[:, 0], part[:, 1]
+            mine = jnp.where(x == 0, first_half, second_half)
+            other = jnp.where(x == 0, second_half, first_half)
+            own[c] = mine
+            rxs[t, c] = other.astype(BF16)
+            rx_copy(t, c).start()
+
+        over_chunks(body)
+
+    def pair_sum(t, c):
+        rx_copy(t, c).wait_recv()
+        total = own[c] + rxr[t, c].astype(F32)
+        own[c] = total
+        rzs[t, c] = total.astype(BF16)
+        for j in range(1, nz):
+            rz_copy(t, c, j).start()
+
+    def line_sum(t, c):
+        total = own[c, z] + dyb[t, c, z, x].astype(F32)
+        for j in range(1, nz):
+            rz_copy(t, c, j).wait_recv()
+            total = total + rzr[t, c, j].astype(F32)
+        res[t, c] = total.astype(BF16)
+        if t + 1 < slots:
+            @pl.when(s > 0)
+            def _():
+                for j in range(nz):
+                    sh_copy(t, c, j).start()
+
+    def hand_over(t, c):
+        for j in range(nz):
+            sh_copy(t, c, j).wait_recv()
+        af_copy(t, c).start()
+
+    def example_mask(t):
+        position = lax.broadcasted_iota(jnp.int32, (tokens, 1), 0)
+        across = lax.broadcasted_iota(jnp.int32, (1, tokens), 1)
+        down, along = [], []
+        start = jnp.int32(0)
+        for e in range(examples):
+            stop = start + lengths_ref[0, t, e]
+            if e == examples - 1:
+                stop = jnp.int32(tokens)
+            down.append((position >= start) & (position < stop))
+            along.append((across >= start) & (across < stop))
+            start = stop
+        return down, along
+
+    def sq_copy(t, j):
+        return pltpu.make_async_remote_copy(sqs.at[t], sqr.at[t, j], sq_send.at[t, j], sq_recv.at[t, j], device_id={"section": s, "tensor": (p + j) % parts}, device_id_type=MESH)
+
+    def squares(t):
+        inputs = xg[t].reshape(tokens, width)
+        grads = jnp.concatenate([dyb[t, c].reshape(tokens, cols) for c in range(chunks)], axis=1)
+        paired = dot(inputs, inputs, NT) * dot(dz[t], dz[t], NT) + dot(h[t], h[t], NT) * dot(grads, grads, NT)
+        down, along = example_mask(t)
+        row = lax.broadcasted_iota(jnp.int32, (8, 128), 0)
+        out = jnp.zeros((8, 128), F32)
+        for e in range(examples):
+            kept = jnp.where(down[e], paired, 0.0)
+            kept = jnp.where(along[e], kept, 0.0)
+            value = jnp.sum(jnp.sum(kept, axis=0, keepdims=True), axis=1, keepdims=True)
+            out = jnp.where(row == e, value, out)
+        sqs[t] = out
+        for j in range(1, parts):
+            sq_copy(t, j).start()
+
+    def out_copy(t, k):
+        source, target = ((h, h_hbm), (dz, dz_hbm), (dyc, dyc_hbm), (xct, xct_hbm))[k]
+        return pltpu.make_async_copy(source.at[t], target.at[t], out_sem.at[t, k])
+
+    def scale(t):
+        total = sqs[t]
+        for j in range(1, parts):
+            sq_copy(t, j).wait_recv()
+            total = total + sqr[t, j]
+        factor = 1.0 / (jnp.sqrt(total / (width * hidden_all)) + GAMMA)
+        down, _ = example_mask(t)
+        per_token = jnp.zeros((tokens, 1), F32)
+        for e in range(examples):
+            per_token = jnp.where(down[e], factor[e:e + 1, 0:1], per_token)
+        scaled = xg[t].reshape(tokens, width).astype(F32) * per_token
+        xct[t] = scaled.T.astype(BF16)
+        for c in range(chunks):
+            dyc[t, :, pl.ds(c * cols, cols)] = (dyb[t, c].reshape(tokens, cols).astype(F32) * per_token).astype(BF16)
+        out_copy(t, 2).start()
+        out_copy(t, 3).start()
+
+    ag_open(0)
+    ag_open(slots)
+    ag_open(1)
+
+    @pl.when(is_last)
+    def _():
+        ag_open(slots + 1)
+
+    for t in range(2, slots):
+        ag_open(t)
+
+    @pl.when(is_last)
+    def _():
+        for t in range(2, slots):
+            ag_open(slots + t)
+
+    ag_forward(0)
+    ag_forward(slots)
+    for k in range(pieces):
+        pltpu.make_async_copy(win_hbm.at[0, :, pl.ds(k * span_in, span_in)], win.at[:, pl.ds(k * span_in, span_in)], w_sem.at[0, k]).wait()
+    for k in range(pieces):
+        pltpu.make_async_copy(wout_hbm.at[0, pl.ds(k * span_out, span_out)], wout.at[pl.ds(k * span_out, span_out)], w_sem.at[1, k]).wait()
+    ag_finish(0)
+    z_tiles(0, 0, tiles)
+    ag_finish(slots)
+    back_all(0)
+
+    for t in range(slots):
+        more = t + 1 < slots
+        partial_dx(t)
+        out_copy(t, 0).start()
+        out_copy(t, 1).start()
+        squares(t)
+        if more:
+            ag_forward(t + 1)
+
+            @pl.when(is_last)
+            def _():
+                ag_forward(slots + t + 1)
+
+        over_chunks(lambda c: pair_sum(t, c))
+        if more:
+            ag_finish(t + 1)
+            z_tiles(t + 1, 0, tiles)
+        scale(t)
+        over_chunks(lambda c: line_sum(t, c))
+        if more:
+            @pl.when(s < sections - 1)
+            def _():
+                over_chunks(lambda c: hand_over(t, c))
+
+            @pl.when(is_last)
+            def _():
+                ag_finish(slots + t + 1)
+
+            for c in range(chunks):
+                @pl.when(s < sections - 1)
+                def _():
+                    af_copy(t, c).wait_recv()
+
+                back_chunk(t + 1, c, 0 if c == 0 else (2 if c == chunks - 1 else 1))
+
+    copies = []
+    for t in range(slots):
+        for c in range(chunks):
+            copy = pltpu.make_async_copy(res.at[t, c], res_hbm.at[t, :, pl.ds(c * cols, cols)], out_sem.at[t, 4 + c])
+            copy.start()
+            copies.append(copy)
+    for t in range(slots):
+        ag_drain(t)
+    ag_drain(slots)
+
+    @pl.when(is_last)
+    def _():
+        for t in range(1, slots):
+            ag_drain(slots + t)
+
+    for t in range(slots):
+        def drain(c):
+            rx_copy(t, c).wait_send()
+            for j in range(1, nz):
+                rz_copy(t, c, j).wait_send()
+
+        over_chunks(drain)
+        for j in range(1, parts):
+            sq_copy(t, j).wait_send()
+        if t + 1 < slots:
+            @pl.when(s > 0)
+            def _():
+                def drain_shift(c):
+                    for j in range(nz):
+                        sh_copy(t, c, j).wait_send()
+
+                over_chunks(drain_shift)
+
+            @pl.when(s < sections - 1)
+            def _():
+                over_chunks(lambda c: af_copy(t, c).wait_send())
+    for t in range(slots):
+        for k in range(4):
+            out_copy(t, k).wait()
+    for copy in copies:
+        copy.wait()
+
+
+def grads_kernel(xct_ref, dyc_ref, h_ref, dz_ref, res_ref, gin_ref, gout_ref, out_ref):
+    slots = xct_ref.shape[0]
+    lhs = jnp.concatenate([xct_ref[t] for t in range(slots)], axis=1)
+    tokens, block = h_ref.shape[1:]
+    dzs = dz_ref[...].reshape(slots * tokens, block)
+    gin_ref[0] = jnp.dot(lhs, dzs, preferred_element_type=F32).astype(BF16)
+    hs = h_ref[...].reshape(slots * tokens, block)
+    dycs = dyc_ref[...].reshape(slots * tokens, dyc_ref.shape[2])
+    gout_ref[0] = dot(hs, dycs, TN).astype(BF16)
+
+    @pl.when(pl.program_id(0) == 0)
+    def _():
+        out_ref[0] = res_ref[...]
+
+
+def fast_device(sections, saved_inputs, slot_index, example_lengths, first_grads, loss_grads, w_in, w_out):
+    parts = lax.axis_size("tensor")
+    slots = loss_grads.shape[0] + 1
+    rows, width = first_grads.shape[1:]
+    local = w_in.shape[2]
+    nz = parts // 2
+    tokens = parts * rows
+    examples = example_lengths.shape[2]
+    chunks = max(1, width // 256)
+    cols = width // chunks
+    cfg = (sections, parts, nz, slots, rows, width, local, chunks, examples, local * parts)
+    hbm = pl.BlockSpec(memory_space=pl.ANY)
+    vmem = pl.BlockSpec(memory_space=pltpu.VMEM)
+    smem = pl.BlockSpec(memory_space=pltpu.SMEM)
+    dma = pltpu.SemaphoreType.DMA
+    sds = jax.ShapeDtypeStruct
+    flops = 2 * tokens * width * local * slots * 3
+    xct, dyc, h, dz, res = pl.pallas_call(
+        functools.partial(chain_kernel, cfg),
+        out_shape=(
+            sds((slots, width, tokens), BF16),
+            sds((slots, tokens, width), BF16),
+            sds((slots, tokens, local), BF16),
+            sds((slots, tokens, local), BF16),
+            sds((slots, rows, width), BF16),
+        ),
+        in_specs=[smem, smem, vmem, vmem, vmem, hbm, hbm],
+        out_specs=[hbm] * 5,
+        scratch_shapes=[
+            pltpu.VMEM((width, local), BF16),
+            pltpu.VMEM((local, width), BF16),
+            pltpu.VMEM((slots, nz, 2, rows, width), BF16),
+            pltpu.VMEM((slots, chunks, nz, 2, rows, cols), BF16),
+            pltpu.VMEM((slots, tokens, local), BF16),
+            pltpu.VMEM((slots, tokens, local), BF16),
+            pltpu.VMEM((tokens, local), F32),
+            pltpu.VMEM((tokens, local), F32),
+            pltpu.VMEM((chunks, nz, rows, cols), F32),
+            pltpu.VMEM((slots, chunks, nz, rows, cols), BF16),
+            pltpu.VMEM((slots, chunks, nz, rows, cols), BF16),
+            pltpu.VMEM((slots, chunks, nz, rows, cols), BF16),
+            pltpu.VMEM((slots, chunks, nz, rows, cols), BF16),
+            pltpu.VMEM((slots, chunks, rows, cols), BF16),
+            pltpu.VMEM((slots, 8, 128), F32),
+            pltpu.VMEM((slots, parts, 8, 128), F32),
+            pltpu.VMEM((slots, width, tokens), BF16),
+            pltpu.VMEM((slots, tokens, width), BF16),
+            dma((2, 4)),
+            dma((2 * slots, nz)), dma((2 * slots, nz)), dma((2 * slots, nz)), dma((2 * slots, nz)),
+            dma((slots, chunks)), dma((slots, chunks)),
+            dma((slots, chunks, nz)), dma((slots, chunks, nz)),
+            dma((slots - 1, chunks, nz)), dma((slots - 1, chunks, nz)),
+            dma((slots - 1, chunks)), dma((slots - 1, chunks)),
+            dma((slots, parts)), dma((slots, parts)),
+            dma((slots, 4 + chunks)),
+        ],
+        compiler_params=pltpu.CompilerParams(collective_id=0, has_side_effects=True, vmem_limit_bytes=60 * 1024 * 1024),
+        cost_estimate=pl.CostEstimate(flops=flops, bytes_accessed=4 * width * local, transcendentals=0),
+        name="chain",
+    )(slot_index, example_lengths, saved_inputs, first_grads, loss_grads, w_in, w_out)
+
+    block = min(512, local)
+    return pl.pallas_call(
+        grads_kernel,
+        grid=(local // block,),
+        out_shape=(
+            sds((1, width, local), BF16),
+            sds((1, local, width), BF16),
+            sds((1, slots, rows, width), BF16),
+        ),
+        in_specs=[
+            pl.BlockSpec((slots, width, tokens), lambda i: (0, 0, 0)),
+            pl.BlockSpec((slots, tokens, width), lambda i: (0, 0, 0)),
+            pl.BlockSpec((slots, tokens, block), lambda i: (0, 0, i)),
+            pl.BlockSpec((slots, tokens, block), lambda i: (0, 0, i)),
+            pl.BlockSpec((slots, rows, width), lambda i: (0, 0, 0)),
+        ],
+        out_specs=[
+            pl.BlockSpec((1, width, block), lambda i: (0, 0, i)),
+            pl.BlockSpec((1, block, width), lambda i: (0, i, 0)),
+            pl.BlockSpec((1, slots, rows, width), lambda i: (0, 0, 0, 0)),
+        ],
+        compiler_params=pltpu.CompilerParams(dimension_semantics=("arbitrary",), vmem_limit_bytes=60 * 1024 * 1024),
+        cost_estimate=pl.CostEstimate(flops=4 * slots * tokens * width * local, bytes_accessed=8 * width * local, transcendentals=0),
+        name="grads",
+    )(xct, dyc, h, dz, res)
 
 
 def shifted(value, axis, steps):
@@ -92,8 +543,17 @@
 
 
 def solution(mesh):
+    sections = mesh.shape["section"]
+    parts = mesh.shape["tensor"]
+
+    def body(saved_inputs, slot_index, example_lengths, first_grads, loss_grads, w_in, w_out):
+        rows, width = first_grads.shape[1:]
+        fits = sections > 2 and parts % 2 == 0 and rows % 16 == 0 and width % 256 == 0 and w_in.shape[2] % 512 == 0 and loss_grads.shape[0] > 0
+        run = functools.partial(fast_device, sections) if fits else per_device
+        return run(saved_inputs, slot_index, example_lengths, first_grads, loss_grads, w_in, w_out)
+
     return jax.shard_map(
-        per_device,
+        body,
         mesh=mesh,
         in_specs=(
             P("section", None, "tensor", None),

time: 229 us -> 135 us (0.59)
  Pallas kernels: 0 us -> 132 us
  matrix products: 95.6 us -> 0 us
  waiting for transfers between devices: 58.5 us -> 0 us
  starting transfers between devices: 41.1 us -> 0 us
  local copies, waits for them, and re-layouts: 15.4 us -> 1.34 us
  other arithmetic: 10.1 us -> 0 us
  between operations: 7.11 us -> 0.64 us
    pallas_call x0 -> x2, Pallas kernels: none -> 132 us  [the longest x1 113 us: fast_device(): pl.pallas_call(functools.partial(chain_kernel, cfg), out_shape=(sds((slot...]
    dot_general x23 -> x0, matrix products: 95.6 us -> none  [the longest x3 24.7 us: per_device(): z = jnp.dot(inputs, first, preferred_element_type=F32)]
    all_to_all x8 -> x0, waiting for transfers between devices: 57.3 us -> none  [the longest x5 44.7 us: spread(): return lax.all_to_all(copies, axis, 0, 0)]
    all_to_all x8 -> x0, starting transfers between devices: 38.5 us -> none  [the longest x5 23.7 us: spread(): return lax.all_to_all(copies, axis, 0, 0)]
    slice x8 -> x0, local copies, waits for them, and re-layouts: 5.71 us -> none  [the longest x1 2.16 us: per_device(): later[:, slot * rows:(slot + 1) * rows].reshape(tokens, width)]
    broadcast_in_dim x5 -> x0, local copies, waits for them, and re-layouts: 4.59 us -> none  [spread(): copies = jnp.broadcast_to(value[None], (lax.axis_size(axis),) + value.shape)]
    reduce_sum x9 -> x0, other arithmetic: 4.5 us -> none  [the longest x3 3.38 us: per_device(): shares = jnp.sum(pieces.astype(F32), axis=0)]
    unnamed x68 -> x1, local copies, waits for them, and re-layouts: 4.07 us -> 1.34 us
  transfers between devices with their start and end apart: 10 -> 0, of which waited for: 7 -> 0; matrix products, arithmetic and copies ran while one was open for 35% -> 0% of each run, Pallas kernels for 0% -> 0%
where the time goes in v1:
time: 135 us; the launch traced here: 134 us
  Pallas kernels  132 us (98%)
    pallas_call x1, Pallas kernels, fast_device(): pl.pallas_call(functools.partial(chain_kernel, cfg), out_shape=(sds((slot...  113 us
    pallas_call x1, Pallas kernels, fast_device(): pl.pallas_call(grads_kernel, grid=(local // block,), out_shape=(sds((1, w...  19.4 us

profile of v1, /device:TPU:0, one launch (start us, length us, event | category | flops | bytes accessed | tf_op | source)
XLA Modules:
  0.0 134.1 jit_solution(6418342982789189481)
XLA Ops:
  0.6 1.3 copy.10.lengths_ref
  2.0 112.8 %chain.1 = (bf16[3,1024,256]{2,1,0:T(8,128)(2,1)}, bf16[3,256,1024]{2,1,0:T(8,128)(2,1)}, bf16[3,256,4096]{2,1,0:T(8,128)(2,1)}, bf16[3,256,4096]{2,1,0:T(8,128)(2,1)}, bf16[3,32,1024]{2,1,0:T(8,128)(2,1)}) custom-call(s32[1,3]{1,0:T(1,128)} %index_ref.1, s32[1,3,2]{2,1,0:T(4,128)} %copy.10.lengths_ref, bf16[1,4,32,1024]{3,2,1,0:T(8,128)(2,1)} %saved_ref.1, ...), custom_call_target="tpu_custom_call" | custom-call | flops 19327352832 | bytes 16777216 | tf_op jit(solution)/shard_map/chain/pallas_call | solution.py:391
  114.7 19.4 %grads.1 = (bf16[1,1024,4096]{2,1,0:T(8,128)(2,1)}, bf16[1,4096,1024]{2,1,0:T(8,128)(2,1)}, bf16[1,3,32,1024]{3,2,1,0:T(8,128)(2,1)}) custom-call(bf16[3,1024,256]{2,1,0:T(8,128)(2,1)} %get-tuple-element.8.xct_ref, bf16[3,256,1024]{2,1,0:T(8,128)(2,1)} %get-tuple-element.9.dyc_ref, bf16[3,256,4096]{2,1,0:T(8,128)(2,1)} %get-tuple-element.10.h_ref, ...), custom_call_target="tpu_custom_call" | custom-call | flops 12884901888 | bytes 33554432 | tf_op jit(solution)/shard_map/grads/pallas_call | solution.py:436

commit v2 on v1

--- a/solution.py
+++ b/solution.py
@@ -22,16 +22,18 @@
 def chain_kernel(
     cfg,
     index_ref, lengths_ref, saved_ref, first_ref, loss_ref, win_hbm, wout_hbm,
-    xct_hbm, dyc_hbm, h_hbm, dz_hbm, res_hbm,
-    win, wout, xg, dyb, h, dz, rbuf, acc, own, rxs, rxr, rzs, rzr, res, sqs, sqr, xct, dyc,
+    gin_ref, gout_ref, res_ref,
+    xg, dyb, h, dz, rbuf, acc, own, rxs, rxr, rzs, rzr, res, sqs, sqr, xct, dyc,
     w_sem, ag_send, ag_recv, fw_send, fw_recv, rx_send, rx_recv, rz_send, rz_recv,
-    sh_send, sh_recv, af_send, af_recv, sq_send, sq_recv, out_sem,
+    sh_send, sh_recv, af_send, af_recv, sq_send, sq_recv,
 ):
     sections, parts, nz, slots, rows, width, local, chunks, examples, hidden_all = cfg
     cols = width // chunks
     tokens = parts * rows
-    tile = min(512, local)
+    win, wout = gin_ref.at[0], gout_ref.at[0]
+    tile = min(2048, local)
     tiles = local // tile
+    span = local // chunks
     s = lax.axis_index("section")
     p = lax.axis_index("tensor")
     z = p // 2
@@ -203,7 +205,7 @@
         down, along = [], []
         start = jnp.int32(0)
         for e in range(examples):
-            stop = start + lengths_ref[0, t, e]
+            stop = start + lengths_ref[0, e, t]
             if e == examples - 1:
                 stop = jnp.int32(tokens)
             down.append((position >= start) & (position < stop))
@@ -230,10 +232,6 @@
         for j in range(1, parts):
             sq_copy(t, j).start()
 
-    def out_copy(t, k):
-        source, target = ((h, h_hbm), (dz, dz_hbm), (dyc, dyc_hbm), (xct, xct_hbm))[k]
-        return pltpu.make_async_copy(source.at[t], target.at[t], out_sem.at[t, k])
-
     def scale(t):
         total = sqs[t]
         for j in range(1, parts):
@@ -248,8 +246,17 @@
         xct[t] = scaled.T.astype(BF16)
         for c in range(chunks):
             dyc[t, :, pl.ds(c * cols, cols)] = (dyb[t, c].reshape(tokens, cols).astype(F32) * per_token).astype(BF16)
-        out_copy(t, 2).start()
-        out_copy(t, 3).start()
+
+    def grad_in_block(i):
+        at = pl.ds(pl.multiple_of(i * span, span), span)
+        lhs = jnp.concatenate([xct[t] for t in range(slots)], axis=1)
+        rhs = jnp.concatenate([dz[t, :, at] for t in range(slots)], axis=0)
+        win[:, at] = jnp.dot(lhs, rhs, preferred_element_type=F32).astype(BF16)
+
+    def grad_out_block(i):
+        at = pl.ds(pl.multiple_of(i * span, span), span)
+        lhs = jnp.concatenate([h[t, :, at] for t in range(slots)], axis=0)
+        wout[at, :] = dot(lhs, dyc[...].reshape(slots * tokens, width), TN).astype(BF16)
 
     ag_open(0)
     ag_open(slots)
@@ -278,47 +285,56 @@
     ag_finish(slots)
     back_all(0)
 
-    for t in range(slots):
-        more = t + 1 < slots
+    for t in range(slots - 1):
         partial_dx(t)
-        out_copy(t, 0).start()
-        out_copy(t, 1).start()
         squares(t)
-        if more:
-            ag_forward(t + 1)
-
-            @pl.when(is_last)
-            def _():
-                ag_forward(slots + t + 1)
+        ag_forward(t + 1)
+
+        @pl.when(is_last)
+        def _():
+            ag_forward(slots + t + 1)
 
         over_chunks(lambda c: pair_sum(t, c))
-        if more:
-            ag_finish(t + 1)
-            z_tiles(t + 1, 0, tiles)
+        ag_finish(t + 1)
+        z_tiles(t + 1, 0, tiles)
         scale(t)
         over_chunks(lambda c: line_sum(t, c))
-        if more:
+
+        @pl.when(s < sections - 1)
+        def _():
+            over_chunks(lambda c: hand_over(t, c))
+
+        @pl.when(is_last)
+        def _():
+            ag_finish(slots + t + 1)
+
+        for c in range(chunks):
             @pl.when(s < sections - 1)
             def _():
-                over_chunks(lambda c: hand_over(t, c))
-
-            @pl.when(is_last)
-            def _():
-                ag_finish(slots + t + 1)
-
-            for c in range(chunks):
-                @pl.when(s < sections - 1)
-                def _():
-                    af_copy(t, c).wait_recv()
-
-                back_chunk(t + 1, c, 0 if c == 0 else (2 if c == chunks - 1 else 1))
-
-    copies = []
+                af_copy(t, c).wait_recv()
+
+            back_chunk(t + 1, c, 0 if c == 0 else (2 if c == chunks - 1 else 1))
+
+    end = slots - 1
+    squares(end)
+    partial_dx(end)
+    scale(end)
+
+    def first_half(c):
+        pair_sum(end, c)
+        grad_in_block(c)
+
+    def second_half(c):
+        grad_out_block(c)
+        line_sum(end, c)
+
+    over_chunks(first_half)
+    over_chunks(second_half)
+
     for t in range(slots):
         for c in range(chunks):
-            copy = pltpu.make_async_copy(res.at[t, c], res_hbm.at[t, :, pl.ds(c * cols, cols)], out_sem.at[t, 4 + c])
-            copy.start()
-            copies.append(copy)
+            res_ref[0, t, :, c * cols:(c + 1) * cols] = res[t, c]
+
     for t in range(slots):
         ag_drain(t)
     ag_drain(slots)
@@ -349,26 +365,23 @@
             @pl.when(s < sections - 1)
             def _():
                 over_chunks(lambda c: af_copy(t, c).wait_send())
-    for t in range(slots):
-        for k in range(4):
-            out_copy(t, k).wait()
+
+
+FLUSH = 4
+
+
+def flush_kernel(gin_ref, gout_ref, res_ref, gin_hbm, gout_hbm, res_hbm, sem):
+    copies = []
+    for k, (source, target) in enumerate(((gin_ref, gin_hbm), (gout_ref, gout_hbm))):
+        step = source.shape[1] // FLUSH
+        for i in range(FLUSH):
+            at = pl.ds(i * step, step)
+            copies.append(pltpu.make_async_copy(source.at[:, at], target.at[:, at], sem.at[k * FLUSH + i]))
+    copies.append(pltpu.make_async_copy(res_ref, res_hbm, sem.at[2 * FLUSH]))
+    for copy in copies:
+        copy.start()
     for copy in copies:
         copy.wait()
-
-
-def grads_kernel(xct_ref, dyc_ref, h_ref, dz_ref, res_ref, gin_ref, gout_ref, out_ref):
-    slots = xct_ref.shape[0]
-    lhs = jnp.concatenate([xct_ref[t] for t in range(slots)], axis=1)
-    tokens, block = h_ref.shape[1:]
-    dzs = dz_ref[...].reshape(slots * tokens, block)
-    gin_ref[0] = jnp.dot(lhs, dzs, preferred_element_type=F32).astype(BF16)
-    hs = h_ref[...].reshape(slots * tokens, block)
-    dycs = dyc_ref[...].reshape(slots * tokens, dyc_ref.shape[2])
-    gout_ref[0] = dot(hs, dycs, TN).astype(BF16)
-
-    @pl.when(pl.program_id(0) == 0)
-    def _():
-        out_ref[0] = res_ref[...]
 
 
 def fast_device(sections, saved_inputs, slot_index, example_lengths, first_grads, loss_grads, w_in, w_out):
@@ -387,21 +400,17 @@
     smem = pl.BlockSpec(memory_space=pltpu.SMEM)
     dma = pltpu.SemaphoreType.DMA
     sds = jax.ShapeDtypeStruct
-    flops = 2 * tokens * width * local * slots * 3
-    xct, dyc, h, dz, res = pl.pallas_call(
+    flops = 2 * tokens * width * local * slots * 5
+    grad_in, grad_out, results = pl.pallas_call(
         functools.partial(chain_kernel, cfg),
         out_shape=(
-            sds((slots, width, tokens), BF16),
-            sds((slots, tokens, width), BF16),
-            sds((slots, tokens, local), BF16),
-            sds((slots, tokens, local), BF16),
-            sds((slots, rows, width), BF16),
+            pltpu.VMEM((1, width, local), BF16),
+            pltpu.VMEM((1, local, width), BF16),
+            pltpu.VMEM((1, slots, rows, width), BF16),
         ),
         in_specs=[smem, smem, vmem, vmem, vmem, hbm, hbm],
-        out_specs=[hbm] * 5,
+        out_specs=[vmem, vmem, vmem],
         scratch_shapes=[
-            pltpu.VMEM((width, local), BF16),
-            pltpu.VMEM((local, width), BF16),
             pltpu.VMEM((slots, nz, 2, rows, width), BF16),
             pltpu.VMEM((slots, chunks, nz, 2, rows, cols), BF16),
             pltpu.VMEM((slots, tokens, local), BF16),
@@ -425,38 +434,26 @@
             dma((slots - 1, chunks, nz)), dma((slots - 1, chunks, nz)),
             dma((slots - 1, chunks)), dma((slots - 1, chunks)),
             dma((slots, parts)), dma((slots, parts)),
-            dma((slots, 4 + chunks)),
         ],
-        compiler_params=pltpu.CompilerParams(collective_id=0, has_side_effects=True, vmem_limit_bytes=60 * 1024 * 1024),
+        compiler_params=pltpu.CompilerParams(collective_id=0, has_side_effects=True, vmem_limit_bytes=44 * 1024 * 1024),
         cost_estimate=pl.CostEstimate(flops=flops, bytes_accessed=4 * width * local, transcendentals=0),
         name="chain",
-    )(slot_index, example_lengths, saved_inputs, first_grads, loss_grads, w_in, w_out)
-
-    block = min(512, local)
+    )(slot_index, jnp.swapaxes(example_lengths, 1, 2), saved_inputs, first_grads, loss_grads, w_in, w_out)
+
     return pl.pallas_call(
-        grads_kernel,
-        grid=(local // block,),
+        flush_kernel,
         out_shape=(
             sds((1, width, local), BF16),
             sds((1, local, width), BF16),
             sds((1, slots, rows, width), BF16),
         ),
-        in_specs=[
-            pl.BlockSpec((slots, width, tokens), lambda i: (0, 0, 0)),
-            pl.BlockSpec((slots, tokens, width), lambda i: (0, 0, 0)),
-            pl.BlockSpec((slots, tokens, block), lambda i: (0, 0, i)),
-            pl.BlockSpec((slots, tokens, block), lambda i: (0, 0, i)),
-            pl.BlockSpec((slots, rows, width), lambda i: (0, 0, 0)),
-        ],
-        out_specs=[
-            pl.BlockSpec((1, width, block), lambda i: (0, 0, i)),
-            pl.BlockSpec((1, block, width), lambda i: (0, i, 0)),
-            pl.BlockSpec((1, slots, rows, width), lambda i: (0, 0, 0, 0)),
-        ],
-        compiler_params=pltpu.CompilerParams(dimension_semantics=("arbitrary",), vmem_limit_bytes=60 * 1024 * 1024),
-        cost_estimate=pl.CostEstimate(flops=4 * slots * tokens * width * local, bytes_accessed=8 * width * local, transcendentals=0),
-        name="grads",
-    )(xct, dyc, h, dz, res)
+        in_specs=[vmem] * 3,
+        out_specs=[hbm] * 3,
+        scratch_shapes=[dma((FLUSH * 2 + 1,))],
+        compiler_params=pltpu.CompilerParams(vmem_limit_bytes=1024 * 1024),
+        cost_estimate=pl.CostEstimate(flops=0, bytes_accessed=8 * width * local, transcendentals=0),
+        name="flush",
+    )(grad_in, grad_out, results)
 
 
 def shifted(value, axis, steps):

time: 135 us -> 117 us (0.87)
  Pallas kernels: 132 us -> 116 us
    pallas_call x2, Pallas kernels: 132 us -> 116 us  [the longest x1 110 us: fast_device(): pl.pallas_call(functools.partial(chain_kernel, cfg), out_shape=(pltpu.VME...]
where the time goes in v2:
time: 117 us
  Pallas kernels  116 us (99%)
    pallas_call x1, Pallas kernels, fast_device(): pl.pallas_call(functools.partial(chain_kernel, cfg), out_shape=(pltpu.VME...  110 us
    pallas_call x1, Pallas kernels, fast_device(): pl.pallas_call(flush_kernel, out_shape=(sds((1, width, local), BF16), sds...  5.94 us

profile of v2, /device:TPU:0, one launch (start us, length us, event | category | flops | bytes accessed | tf_op | source)
XLA Modules:
  0.0 117.0 jit_solution(15691698594330138375)
XLA Ops:
  0.6 110.3 %chain.1 = (bf16[1,1024,4096]{2,1,0:T(8,128)(2,1)S(1)}, bf16[1,4096,1024]{2,1,0:T(8,128)(2,1)S(1)}, bf16[1,3,32,1024]{3,2,1,0:T(8,128)(2,1)S(1)}) custom-call(s32[1,3]{1,0:T(1,128)} %index_ref.1, s32[1,2,3]{2,1,0:T(2,128)} %bitcast.1, bf16[1,4,32,1024]{3,2,1,0:T(8,128)(2,1)} %saved_ref.1, bf16[1,32,1024]{2,1,0:T(8,128)(2,1)} %first_ref.1, ...), custom_call_target="tpu_custom_call" | custom-call | flops 32212254720 | bytes 16777216 | tf_op jit(solution)/shard_map/chain/pallas_call | solution.py:404
  110.9 5.9 %flush.1 = (bf16[1,1024,4096]{2,1,0:T(8,128)(2,1)}, bf16[1,4096,1024]{2,1,0:T(8,128)(2,1)}, bf16[1,3,32,1024]{3,2,1,0:T(8,128)(2,1)}) custom-call(bf16[1,1024,4096]{2,1,0:T(8,128)(2,1)S(1)} %get-tuple-element.6.gin_ref, bf16[1,4096,1024]{2,1,0:T(8,128)(2,1)S(1)} %get-tuple-element.7.gout_ref, bf16[1,3,32,1024]{3,2,1,0:T(8,128)(2,1)S(1)} %get-tuple-element.8.res_ref), custom_call_target="tpu_custom_call" | custom-call | bytes 33554432 | tf_op jit(solution)/shard_map/flush/pallas_call | solution.py:443

commit v3 on v2

--- a/solution.py
+++ b/solution.py
@@ -21,18 +21,19 @@
 
 def chain_kernel(
     cfg,
-    index_ref, lengths_ref, saved_ref, first_ref, loss_ref, win_hbm, wout_hbm,
-    gin_ref, gout_ref, res_ref,
-    xg, dyb, h, dz, rbuf, acc, own, rxs, rxr, rzs, rzr, res, sqs, sqr, xct, dyc,
+    index_hbm, lengths_hbm, saved_hbm, first_hbm, loss_hbm, win_hbm, wout_hbm,
+    gin_ref, gout_ref, h, dyc, res_ref,
+    xg, dyb, dz, rbuf, acc, gxs, ghs, own, rxs, rxr, rzs, rzr, res, sqs, sqr, xct,
+    index_ref, lengths_ref, saved_ref, in_sem,
     w_sem, ag_send, ag_recv, fw_send, fw_recv, rx_send, rx_recv, rz_send, rz_recv,
     sh_send, sh_recv, af_send, af_recv, sq_send, sq_recv,
 ):
-    sections, parts, nz, slots, rows, width, local, chunks, examples, hidden_all = cfg
+    sections, parts, nz, slots, rows, width, local, chunks, sub, ready, examples, hidden_all = cfg
     cols = width // chunks
+    count = chunks * sub
+    part_cols = cols // sub
     tokens = parts * rows
     win, wout = gin_ref.at[0], gout_ref.at[0]
-    tile = min(2048, local)
-    tiles = local // tile
     span = local // chunks
     s = lax.axis_index("section")
     p = lax.axis_index("tensor")
@@ -47,6 +48,26 @@
     def behind(j):
         return {"section": s - 1, "tensor": ((z + j) % nz) * 2 + x}
 
+    index_in = pltpu.make_async_copy(index_hbm, index_ref, in_sem.at[0])
+    lengths_in = pltpu.make_async_copy(lengths_hbm, lengths_ref, in_sem.at[1])
+    saved_in = pltpu.make_async_copy(saved_hbm.at[0], saved_ref, in_sem.at[2])
+    index_in.start()
+    saved_in.start()
+    lengths_in.start()
+
+    def grads_in(t, c):
+        source = first_hbm.at[0] if t == 0 else loss_hbm.at[t - 1]
+        return pltpu.make_async_copy(source.at[:, c * part_cols:(c + 1) * part_cols], dyb.at[t, c, z, x], in_sem.at[3 + t * count + c])
+
+    for c in range(count):
+        grads_in(0, c).start()
+
+    @pl.when(is_last)
+    def _():
+        for t in range(1, slots):
+            for c in range(count):
+                grads_in(t, c).start()
+
     pieces = 4
     span_in, span_out = local // pieces, local // pieces
     for k in range(pieces):
@@ -54,24 +75,27 @@
     for k in range(pieces):
         pltpu.make_async_copy(wout_hbm.at[0, pl.ds(k * span_out, span_out)], wout.at[pl.ds(k * span_out, span_out)], w_sem.at[1, k]).start()
 
+    barrier = pltpu.get_barrier_semaphore()
+    for j in range(1, parts):
+        pl.semaphore_signal(barrier, inc=1, device_id={"section": s, "tensor": (p + j) % parts}, device_id_type=MESH)
+
+    for side in (1, sections - 1):
+        for j in range(nz):
+            pl.semaphore_signal(barrier, inc=1, device_id={"section": (s + side) % sections, "tensor": ((z + j) % nz) * 2 + x}, device_id_type=MESH)
+    index_in.wait()
+    saved_in.wait()
     for t in range(slots):
-        xg[t, z, x] = saved_ref[0, index_ref[0, t]]
-    for c in range(chunks):
-        dyb[0, c, z, x] = first_ref[0, :, pl.ds(c * cols, cols)]
+        xg[t, z, x] = saved_ref[index_ref[0, t]]
+    for c in range(count):
+        grads_in(0, c).wait()
+    lengths_in.wait()
 
     @pl.when(is_last)
     def _():
         for t in range(1, slots):
-            for c in range(chunks):
-                dyb[t, c, z, x] = loss_ref[t - 1, :, pl.ds(c * cols, cols)]
-
-    barrier = pltpu.get_barrier_semaphore()
-    for j in range(1, parts):
-        pl.semaphore_signal(barrier, inc=1, device_id={"section": s, "tensor": (p + j) % parts}, device_id_type=MESH)
-
-    for side in (1, sections - 1):
-        for j in range(nz):
-            pl.semaphore_signal(barrier, inc=1, device_id={"section": (s + side) % sections, "tensor": ((z + j) % nz) * 2 + x}, device_id_type=MESH)
+            for c in range(count):
+                grads_in(t, c).wait()
+
     pl.semaphore_wait(barrier, parts - 1 + 2 * nz)
 
     def block(k, source):
@@ -106,31 +130,27 @@
                 ag_copy(k, j, False).wait_send()
             ag_copy(k, j, True).wait_send()
 
-    def z_tiles(t, lo, hi):
+    def grads_of(t, lo, hi):
+        return jnp.concatenate([dyb[t, c].reshape(tokens, part_cols) for c in range(lo, hi)], axis=1)
+
+    def z_tile(t, i, size):
+        at = pl.ds(pl.multiple_of(i * size, size), size)
+        zz = jnp.dot(xg[t].reshape(tokens, width), win[:, at], preferred_element_type=F32)
+        r = jnp.maximum(zz, 0.0)
+        rbuf[:, at] = r
+        h[t, :, at] = (r * r).astype(BF16)
+
+    def back_tile(t, i, size):
+        at = pl.ds(pl.multiple_of(i * size, size), size)
+        dh = dot(grads_of(t, 0, count), wout[at, :], NT)
+        dz[t, :, at] = (2.0 * rbuf[:, at] * dh).astype(BF16)
+
+    def back_chunk(t, c, mode):
+        size = min(2048, local)
+
         def body(i, carry):
-            at = pl.ds(pl.multiple_of(i * tile, tile), tile)
-            zz = jnp.dot(xg[t].reshape(tokens, width), win[:, at], preferred_element_type=F32)
-            r = jnp.maximum(zz, 0.0)
-            rbuf[:, at] = r
-            h[t, :, at] = (r * r).astype(BF16)
-            return carry
-
-        lax.fori_loop(lo, hi, body, 0)
-
-    def back_all(t):
-        def body(i, carry):
-            at = pl.ds(pl.multiple_of(i * tile, tile), tile)
-            grads = jnp.concatenate([dyb[t, c].reshape(tokens, cols) for c in range(chunks)], axis=1)
-            dh = dot(grads, wout[at, :], NT)
-            dz[t, :, at] = (2.0 * rbuf[:, at] * dh).astype(BF16)
-            return carry
-
-        lax.fori_loop(0, tiles, body, 0)
-
-    def back_chunk(t, c, mode):
-        def body(i, carry):
-            at = pl.ds(pl.multiple_of(i * tile, tile), tile)
-            dh = dot(dyb[t, c].reshape(tokens, cols), wout[at, c * cols:(c + 1) * cols], NT)
+            at = pl.ds(pl.multiple_of(i * size, size), size)
+            dh = dot(grads_of(t, c * sub, (c + 1) * sub), wout[at, c * cols:(c + 1) * cols], NT)
             if mode > 0:
                 dh = dh + acc[:, at]
             if mode < 2:
@@ -139,7 +159,7 @@
                 dz[t, :, at] = (2.0 * rbuf[:, at] * dh).astype(BF16)
             return carry
 
-        lax.fori_loop(0, tiles, body, 0)
+        lax.fori_loop(0, local // size, body, 0)
 
     def rx_copy(t, c):
         return pltpu.make_async_remote_copy(rxs.at[t, c], rxr.at[t, c], rx_send.at[t, c], rx_recv.at[t, c], device_id=partner, device_id_type=MESH)
@@ -154,25 +174,27 @@
         ref = dyb.at[t + 1, c, :, x]
         return pltpu.make_async_remote_copy(ref, ref, af_send.at[t, c], af_recv.at[t, c], device_id=partner, device_id_type=MESH)
 
-    def over_chunks(body):
+    def over(lo, hi, body):
         def step(c, carry):
             body(c)
             return carry
 
-        lax.fori_loop(0, chunks, step, 0)
+        lax.fori_loop(lo, hi, step, 0)
 
     def partial_dx(t):
         def body(c):
             wide = win[pl.ds(pl.multiple_of(c * cols, cols), cols), :]
-            part = dot(dz[t], wide, NT).reshape(nz, 2, rows, cols)
-            first_half, second_half = part[:, 0], part[:, 1]
-            mine = jnp.where(x == 0, first_half, second_half)
-            other = jnp.where(x == 0, second_half, first_half)
-            own[c] = mine
-            rxs[t, c] = other.astype(BF16)
-            rx_copy(t, c).start()
-
-        over_chunks(body)
+            whole = dot(dz[t], wide, NT)
+            for u in range(sub):
+                part = whole[:, u * part_cols:(u + 1) * part_cols].reshape(nz, 2, rows, part_cols)
+                first_half, second_half = part[:, 0], part[:, 1]
+                mine = jnp.where(x == 0, first_half, second_half)
+                other = jnp.where(x == 0, second_half, first_half)
+                own[c * sub + u] = mine
+                rxs[t, c * sub + u] = other.astype(BF16)
+                rx_copy(t, c * sub + u).start()
+
+        over(0, chunks, body)
 
     def pair_sum(t, c):
         rx_copy(t, c).wait_recv()
@@ -216,10 +238,14 @@
     def sq_copy(t, j):
         return pltpu.make_async_remote_copy(sqs.at[t], sqr.at[t, j], sq_send.at[t, j], sq_recv.at[t, j], device_id={"section": s, "tensor": (p + j) % parts}, device_id_type=MESH)
 
+    def grams(t):
+        inputs = xg[t].reshape(tokens, width)
+        gxs[...] = dot(inputs, inputs, NT)
+        ghs[...] = dot(h[t], h[t], NT)
+
     def squares(t):
-        inputs = xg[t].reshape(tokens, width)
-        grads = jnp.concatenate([dyb[t, c].reshape(tokens, cols) for c in range(chunks)], axis=1)
-        paired = dot(inputs, inputs, NT) * dot(dz[t], dz[t], NT) + dot(h[t], h[t], NT) * dot(grads, grads, NT)
+        grads = grads_of(t, 0, count)
+        paired = gxs[...] * dot(dz[t], dz[t], NT) + ghs[...] * dot(grads, grads, NT)
         down, along = example_mask(t)
         row = lax.broadcasted_iota(jnp.int32, (8, 128), 0)
         out = jnp.zeros((8, 128), F32)
@@ -232,7 +258,7 @@
         for j in range(1, parts):
             sq_copy(t, j).start()
 
-    def scale(t):
+    def factors(t):
         total = sqs[t]
         for j in range(1, parts):
             sq_copy(t, j).wait_recv()
@@ -242,67 +268,88 @@
         per_token = jnp.zeros((tokens, 1), F32)
         for e in range(examples):
             per_token = jnp.where(down[e], factor[e:e + 1, 0:1], per_token)
-        scaled = xg[t].reshape(tokens, width).astype(F32) * per_token
-        xct[t] = scaled.T.astype(BF16)
-        for c in range(chunks):
-            dyc[t, :, pl.ds(c * cols, cols)] = (dyb[t, c].reshape(tokens, cols).astype(F32) * per_token).astype(BF16)
+        return per_token
+
+    def scale(t, k, per_token):
+        at = slice(k * part_cols, (k + 1) * part_cols)
+        scaled = xg[t, :, :, :, at].reshape(tokens, part_cols).astype(F32) * per_token
+        xct[t, at] = scaled.T.astype(BF16)
+        dyc[t, :, at] = (dyb[t, k].reshape(tokens, part_cols).astype(F32) * per_token).astype(BF16)
 
     def grad_in_block(i):
-        at = pl.ds(pl.multiple_of(i * span, span), span)
+        at = pl.ds(i * span, span)
         lhs = jnp.concatenate([xct[t] for t in range(slots)], axis=1)
         rhs = jnp.concatenate([dz[t, :, at] for t in range(slots)], axis=0)
         win[:, at] = jnp.dot(lhs, rhs, preferred_element_type=F32).astype(BF16)
 
     def grad_out_block(i):
-        at = pl.ds(pl.multiple_of(i * span, span), span)
+        at = pl.ds(i * span, span)
         lhs = jnp.concatenate([h[t, :, at] for t in range(slots)], axis=0)
         wout[at, :] = dot(lhs, dyc[...].reshape(slots * tokens, width), TN).astype(BF16)
 
+    end = slots - 1
     ag_open(0)
     ag_open(slots)
-    ag_open(1)
-
-    @pl.when(is_last)
-    def _():
-        ag_open(slots + 1)
-
-    for t in range(2, slots):
-        ag_open(t)
-
-    @pl.when(is_last)
-    def _():
-        for t in range(2, slots):
-            ag_open(slots + t)
+    if end > 0:
+        ag_open(1)
+
+        @pl.when(is_last)
+        def _():
+            ag_open(slots + 1)
 
     ag_forward(0)
     ag_forward(slots)
     for k in range(pieces):
         pltpu.make_async_copy(win_hbm.at[0, :, pl.ds(k * span_in, span_in)], win.at[:, pl.ds(k * span_in, span_in)], w_sem.at[0, k]).wait()
+    ag_finish(0)
+    over(0, 2, lambda i: z_tile(0, i, local // 2))
+    grams(0)
     for k in range(pieces):
         pltpu.make_async_copy(wout_hbm.at[0, pl.ds(k * span_out, span_out)], wout.at[pl.ds(k * span_out, span_out)], w_sem.at[1, k]).wait()
-    ag_finish(0)
-    z_tiles(0, 0, tiles)
     ag_finish(slots)
-    back_all(0)
-
-    for t in range(slots - 1):
+    over(0, 2, lambda i: back_tile(0, i, local // 2))
+
+    for t in range(end):
         partial_dx(t)
+        ag_forward(t + 1)
+        if t > 0:
+            grams(t)
         squares(t)
-        ag_forward(t + 1)
+        over(0, count, lambda k: pair_sum(t, k))
 
         @pl.when(is_last)
         def _():
             ag_forward(slots + t + 1)
 
-        over_chunks(lambda c: pair_sum(t, c))
+        per_token = None
+        for k in range(count):
+            line_sum(t, k)
+            if k == 1:
+                per_token = factors(t)
+            if k > 1:
+                scale(t, k - 2, per_token)
+        if t + 2 < slots:
+            ag_open(t + 2)
+
+            @pl.when(is_last)
+            def _():
+                ag_open(slots + t + 2)
+
+        for k in range(count - 2, count):
+            scale(t, k, per_token)
         ag_finish(t + 1)
-        z_tiles(t + 1, 0, tiles)
-        scale(t)
-        over_chunks(lambda c: line_sum(t, c))
-
-        @pl.when(s < sections - 1)
-        def _():
-            over_chunks(lambda c: hand_over(t, c))
+
+        def tile_and_hand(c):
+            @pl.when(s < sections - 1)
+            def _():
+                for u in range(sub):
+                    hand_over(t, c * sub + u)
+
+            z_tile(t + 1, c, span)
+
+        over(0, chunks, tile_and_hand)
+        if t + 1 == end:
+            grams(end)
 
         @pl.when(is_last)
         def _():
@@ -311,29 +358,28 @@
         for c in range(chunks):
             @pl.when(s < sections - 1)
             def _():
-                af_copy(t, c).wait_recv()
+                for u in range(sub):
+                    af_copy(t, c * sub + u).wait_recv()
 
             back_chunk(t + 1, c, 0 if c == 0 else (2 if c == chunks - 1 else 1))
 
-    end = slots - 1
     squares(end)
     partial_dx(end)
-    scale(end)
-
-    def first_half(c):
-        pair_sum(end, c)
+    per_token = factors(end)
+    for k in range(count):
+        scale(end, k, per_token)
+    for c in range(chunks):
+        for k in range(count):
+            if min(chunks - 1, (k + 2) // 3) == c:
+                pair_sum(end, k)
         grad_in_block(c)
-
-    def second_half(c):
-        grad_out_block(c)
-        line_sum(end, c)
-
-    over_chunks(first_half)
-    over_chunks(second_half)
+    for i in range(ready):
+        grad_out_block(i)
+    over(0, count, lambda k: line_sum(end, k))
 
     for t in range(slots):
-        for c in range(chunks):
-            res_ref[0, t, :, c * cols:(c + 1) * cols] = res[t, c]
+        for c in range(count):
+            res_ref[0, t, :, c * part_cols:(c + 1) * part_cols] = res[t, c]
 
     for t in range(slots):
         ag_drain(t)
@@ -350,7 +396,7 @@
             for j in range(1, nz):
                 rz_copy(t, c, j).wait_send()
 
-        over_chunks(drain)
+        over(0, count, drain)
         for j in range(1, parts):
             sq_copy(t, j).wait_send()
         if t + 1 < slots:
@@ -360,26 +406,36 @@
                     for j in range(nz):
                         sh_copy(t, c, j).wait_send()
 
-                over_chunks(drain_shift)
+                over(0, count, drain_shift)
 
             @pl.when(s < sections - 1)
             def _():
-                over_chunks(lambda c: af_copy(t, c).wait_send())
-
-
-FLUSH = 4
-
-
-def flush_kernel(gin_ref, gout_ref, res_ref, gin_hbm, gout_hbm, res_hbm, sem):
+                over(0, count, lambda c: af_copy(t, c).wait_send())
+
+
+def finish_kernel(cfg, gin_ref, gout_ref, h, dyc, res_ref, gin_hbm, gout_hbm, res_hbm, made, sem):
+    blocks, ready = cfg
+    slots, tokens, local = h.shape
+    width = dyc.shape[2]
+    span = local // blocks
+    step = width // blocks
     copies = []
-    for k, (source, target) in enumerate(((gin_ref, gin_hbm), (gout_ref, gout_hbm))):
-        step = source.shape[1] // FLUSH
-        for i in range(FLUSH):
-            at = pl.ds(i * step, step)
-            copies.append(pltpu.make_async_copy(source.at[:, at], target.at[:, at], sem.at[k * FLUSH + i]))
-    copies.append(pltpu.make_async_copy(res_ref, res_hbm, sem.at[2 * FLUSH]))
+    for i in range(ready):
+        at = pl.ds(i * span, span)
+        copies.append(pltpu.make_async_copy(gout_ref.at[0, at], gout_hbm.at[0, at], sem.at[1, i]))
+    for i in range(blocks):
+        at = pl.ds(i * step, step)
+        copies.append(pltpu.make_async_copy(gin_ref.at[0, at], gin_hbm.at[0, at], sem.at[0, i]))
+    copies.append(pltpu.make_async_copy(res_ref, res_hbm, sem.at[2, 0]))
     for copy in copies:
         copy.start()
+    for i in range(ready, blocks):
+        at = pl.ds(i * span, span)
+        lhs = jnp.concatenate([h[t, :, at] for t in range(slots)], axis=0)
+        made[i - ready] = dot(lhs, dyc[...].reshape(slots * tokens, width), TN).astype(BF16)
+        copy = pltpu.make_async_copy(made.at[i - ready], gout_hbm.at[0, at], sem.at[1, i])
+        copy.start()
+        copies.append(copy)
     for copy in copies:
         copy.wait()
 
@@ -393,67 +449,75 @@
     tokens = parts * rows
     examples = example_lengths.shape[2]
     chunks = max(1, width // 256)
-    cols = width // chunks
-    cfg = (sections, parts, nz, slots, rows, width, local, chunks, examples, local * parts)
+    sub = 2
+    ready = min(1, chunks)
+    count = chunks * sub
+    part_cols = width // count
+    cfg = (sections, parts, nz, slots, rows, width, local, chunks, sub, ready, examples, local * parts)
     hbm = pl.BlockSpec(memory_space=pl.ANY)
     vmem = pl.BlockSpec(memory_space=pltpu.VMEM)
-    smem = pl.BlockSpec(memory_space=pltpu.SMEM)
     dma = pltpu.SemaphoreType.DMA
     sds = jax.ShapeDtypeStruct
     flops = 2 * tokens * width * local * slots * 5
-    grad_in, grad_out, results = pl.pallas_call(
+    grad_in, grad_out, hidden, scaled, results = pl.pallas_call(
         functools.partial(chain_kernel, cfg),
         out_shape=(
             pltpu.VMEM((1, width, local), BF16),
             pltpu.VMEM((1, local, width), BF16),
+            pltpu.VMEM((slots, tokens, local), BF16),
+            pltpu.VMEM((slots, tokens, width), BF16),
             pltpu.VMEM((1, slots, rows, width), BF16),
         ),
-        in_specs=[smem, smem, vmem, vmem, vmem, hbm, hbm],
-        out_specs=[vmem, vmem, vmem],
+        in_specs=[pl.BlockSpec(memory_space=pltpu.HBM)] * 7,
+        out_specs=[vmem] * 5,
         scratch_shapes=[
             pltpu.VMEM((slots, nz, 2, rows, width), BF16),
-            pltpu.VMEM((slots, chunks, nz, 2, rows, cols), BF16),
-            pltpu.VMEM((slots, tokens, local), BF16),
+            pltpu.VMEM((slots, count, nz, 2, rows, part_cols), BF16),
             pltpu.VMEM((slots, tokens, local), BF16),
             pltpu.VMEM((tokens, local), F32),
             pltpu.VMEM((tokens, local), F32),
-            pltpu.VMEM((chunks, nz, rows, cols), F32),
-            pltpu.VMEM((slots, chunks, nz, rows, cols), BF16),
-            pltpu.VMEM((slots, chunks, nz, rows, cols), BF16),
-            pltpu.VMEM((slots, chunks, nz, rows, cols), BF16),
-            pltpu.VMEM((slots, chunks, nz, rows, cols), BF16),
-            pltpu.VMEM((slots, chunks, rows, cols), BF16),
+            pltpu.VMEM((tokens, tokens), F32),
+            pltpu.VMEM((tokens, tokens), F32),
+            pltpu.VMEM((count, nz, rows, part_cols), F32),
+            pltpu.VMEM((slots, count, nz, rows, part_cols), BF16),
+            pltpu.VMEM((slots, count, nz, rows, part_cols), BF16),
+            pltpu.VMEM((slots, count, nz, rows, part_cols), BF16),
+            pltpu.VMEM((slots, count, nz, rows, part_cols), BF16),
+            pltpu.VMEM((slots, count, rows, part_cols), BF16),
             pltpu.VMEM((slots, 8, 128), F32),
             pltpu.VMEM((slots, parts, 8, 128), F32),
             pltpu.VMEM((slots, width, tokens), BF16),
-            pltpu.VMEM((slots, tokens, width), BF16),
+            pltpu.SMEM(slot_index.shape, jnp.int32),
+            pltpu.SMEM((1, examples, slots), jnp.int32),
+            pltpu.VMEM(saved_inputs.shape[1:], BF16),
+            dma((3 + slots * count,)),
             dma((2, 4)),
             dma((2 * slots, nz)), dma((2 * slots, nz)), dma((2 * slots, nz)), dma((2 * slots, nz)),
-            dma((slots, chunks)), dma((slots, chunks)),
-            dma((slots, chunks, nz)), dma((slots, chunks, nz)),
-            dma((slots - 1, chunks, nz)), dma((slots - 1, chunks, nz)),
-            dma((slots - 1, chunks)), dma((slots - 1, chunks)),
+            dma((slots, count)), dma((slots, count)),
+            dma((slots, count, nz)), dma((slots, count, nz)),
+            dma((slots - 1, count, nz)), dma((slots - 1, count, nz)),
+            dma((slots - 1, count)), dma((slots - 1, count)),
             dma((slots, parts)), dma((slots, parts)),
         ],
-        compiler_params=pltpu.CompilerParams(collective_id=0, has_side_effects=True, vmem_limit_bytes=44 * 1024 * 1024),
+        compiler_params=pltpu.CompilerParams(collective_id=0, has_side_effects=True, vmem_limit_bytes=36 * 1024 * 1024),
         cost_estimate=pl.CostEstimate(flops=flops, bytes_accessed=4 * width * local, transcendentals=0),
         name="chain",
     )(slot_index, jnp.swapaxes(example_lengths, 1, 2), saved_inputs, first_grads, loss_grads, w_in, w_out)
 
     return pl.pallas_call(
-        flush_kernel,
+        functools.partial(finish_kernel, (chunks, ready)),
         out_shape=(
             sds((1, width, local), BF16),
             sds((1, local, width), BF16),
             sds((1, slots, rows, width), BF16),
         ),
-        in_specs=[vmem] * 3,
+        in_specs=[vmem] * 5,
         out_specs=[hbm] * 3,
-        scratch_shapes=[dma((FLUSH * 2 + 1,))],
-        compiler_params=pltpu.CompilerParams(vmem_limit_bytes=1024 * 1024),
-        cost_estimate=pl.CostEstimate(flops=0, bytes_accessed=8 * width * local, transcendentals=0),
-        name="flush",
-    )(grad_in, grad_out, results)
+        scratch_shapes=[pltpu.VMEM((chunks - ready, local // chunks, width), BF16), dma((3, chunks))],
+        compiler_params=pltpu.CompilerParams(vmem_limit_bytes=8 * 1024 * 1024),
+        cost_estimate=pl.CostEstimate(flops=2 * slots * tokens * width * local, bytes_accessed=8 * width * local, transcendentals=0),
+        name="finish",
+    )(grad_in, grad_out, hidden, scaled, results)
 
 
 def shifted(value, axis, steps):

time: 117 us -> 107 us (0.915); the launches traced: 117 us -> 106 us
  Pallas kernels: 116 us -> 105 us
    pallas_call x1, Pallas kernels: 110 us -> 98.4 us  [fast_device(): pl.pallas_call(functools.partial(chain_kernel, cfg), out_shape=(pltpu.VME...]
where the time goes in v3:
time: 107 us; the launch traced here: 106 us
  Pallas kernels  105 us (98%)
    pallas_call x1, Pallas kernels, fast_device(): pl.pallas_call(functools.partial(chain_kernel, cfg), out_shape=(pltpu.VME...  98.4 us
    pallas_call x1, Pallas kernels, fast_device(): pl.pallas_call(functools.partial(finish_kernel, (chunks, ready)), out_sha...  6.51 us

profile of v3, /device:TPU:0, one launch (start us, length us, event | category | flops | bytes accessed | tf_op | source)
XLA Modules:
  0.0 105.7 jit_solution(2636851482161533884)
XLA Ops:
  0.6 98.4 %chain.1 = (bf16[1,1024,4096]{2,1,0:T(8,128)(2,1)S(1)}, bf16[1,4096,1024]{2,1,0:T(8,128)(2,1)S(1)}, bf16[3,256,4096]{2,1,0:T(8,128)(2,1)S(1)}, bf16[3,256,1024]{...) custom-call(s32[1,3]{1,0:T(1,128)} %index_hbm.1, s32[1,2,3]{2,1,0:T(2,128)} %bitcast.1, bf16[1,4,32,1024]{3,2,1,0:T(8,128)(2,1)} %saved_hbm.1, ...), custom_call_target="tpu_custom_call" | custom-call | flops 32212254720 | bytes 16777216 | tf_op jit(solution)/shard_map/chain/pallas_call | solution.py:462
  99.0 6.5 %finish.1 = (bf16[1,1024,4096]{2,1,0:T(8,128)(2,1)}, bf16[1,4096,1024]{2,1,0:T(8,128)(2,1)}, bf16[1,3,32,1024]{3,2,1,0:T(8,128)(2,1)}) custom-call(bf16[1,1024,4096]{2,1,0:T(8,128)(2,1)S(1)} %get-tuple-element.8.gin_ref, bf16[1,4096,1024]{2,1,0:T(8,128)(2,1)S(1)} %get-tuple-element.9.gout_ref, bf16[3,256,4096]{2,1,0:T(8,128)(2,1)S(1)} %get-tuple-element.10.h, ...), custom_call_target="tpu_custom_call" | custom-call | flops 6442450944 | bytes 33554432 | tf_op jit(solution)/shard_map/finish/pallas_call | solution.py:507

commit v4 on v3

--- a/solution.py
+++ b/solution.py
@@ -449,7 +449,7 @@
     tokens = parts * rows
     examples = example_lengths.shape[2]
     chunks = max(1, width // 256)
-    sub = 2
+    sub = 1
     ready = min(1, chunks)
     count = chunks * sub
     part_cols = width // count

time: 107 us -> 104 us (0.972)
  Pallas kernels: 105 us -> 103 us
    pallas_call x1, Pallas kernels: 98.4 us -> 96.3 us  [fast_device(): pl.pallas_call(functools.partial(chain_kernel, cfg), out_shape=(pltpu.VME...]
where the time goes in v4:
time: 104 us
  Pallas kernels  103 us (99%)
    pallas_call x1, Pallas kernels, fast_device(): pl.pallas_call(functools.partial(chain_kernel, cfg), out_shape=(pltpu.VME...  96.3 us
    pallas_call x1, Pallas kernels, fast_device(): pl.pallas_call(functools.partial(finish_kernel, (chunks, ready)), out_sha...  6.51 us

profile of v4, /device:TPU:0, one launch (start us, length us, event | category | flops | bytes accessed | tf_op | source)
XLA Modules:
  0.0 103.6 jit_solution(15448865565444806749)
XLA Ops:
  0.6 96.3 %chain.1 = (bf16[1,1024,4096]{2,1,0:T(8,128)(2,1)S(1)}, bf16[1,4096,1024]{2,1,0:T(8,128)(2,1)S(1)}, bf16[3,256,4096]{2,1,0:T(8,128)(2,1)S(1)}, bf16[3,256,1024]{...) custom-call(s32[1,3]{1,0:T(1,128)} %index_hbm.1, s32[1,2,3]{2,1,0:T(2,128)} %bitcast.1, bf16[1,4,32,1024]{3,2,1,0:T(8,128)(2,1)} %saved_hbm.1, ...), custom_call_target="tpu_custom_call" | custom-call | flops 32212254720 | bytes 16777216 | tf_op jit(solution)/shard_map/chain/pallas_call | solution.py:462
  96.9 6.5 %finish.1 = (bf16[1,1024,4096]{2,1,0:T(8,128)(2,1)}, bf16[1,4096,1024]{2,1,0:T(8,128)(2,1)}, bf16[1,3,32,1024]{3,2,1,0:T(8,128)(2,1)}) custom-call(bf16[1,1024,4096]{2,1,0:T(8,128)(2,1)S(1)} %get-tuple-element.8.gin_ref, bf16[1,4096,1024]{2,1,0:T(8,128)(2,1)S(1)} %get-tuple-element.9.gout_ref, bf16[3,256,4096]{2,1,0:T(8,128)(2,1)S(1)} %get-tuple-element.10.h, ...), custom_call_target="tpu_custom_call" | custom-call | flops 6442450944 | bytes 33554432 | tf_op jit(solution)/shard_map/finish/pallas_call | solution.py:507

commit v5 on v4

--- a/solution.py
+++ b/solution.py
@@ -290,6 +290,8 @@
     end = slots - 1
     ag_open(0)
     ag_open(slots)
+    ag_forward(0)
+    ag_forward(slots)
     if end > 0:
         ag_open(1)
 
@@ -297,8 +299,6 @@
         def _():
             ag_open(slots + 1)
 
-    ag_forward(0)
-    ag_forward(slots)
     for k in range(pieces):
         pltpu.make_async_copy(win_hbm.at[0, :, pl.ds(k * span_in, span_in)], win.at[:, pl.ds(k * span_in, span_in)], w_sem.at[0, k]).wait()
     ag_finish(0)
@@ -311,10 +311,10 @@
 
     for t in range(end):
         partial_dx(t)
-        ag_forward(t + 1)
         if t > 0:
             grams(t)
         squares(t)
+        ag_forward(t + 1)
         over(0, count, lambda k: pair_sum(t, k))
 
         @pl.when(is_last)
@@ -328,13 +328,6 @@
                 per_token = factors(t)
             if k > 1:
                 scale(t, k - 2, per_token)
-        if t + 2 < slots:
-            ag_open(t + 2)
-
-            @pl.when(is_last)
-            def _():
-                ag_open(slots + t + 2)
-
         for k in range(count - 2, count):
             scale(t, k, per_token)
         ag_finish(t + 1)
@@ -348,6 +341,13 @@
             z_tile(t + 1, c, span)
 
         over(0, chunks, tile_and_hand)
+        if t + 2 < slots:
+            ag_open(t + 2)
+
+            @pl.when(is_last)
+            def _():
+                ag_open(slots + t + 2)
+
         if t + 1 == end:
             grams(end)
 

time: 104 us -> 100 us (0.962)
  Pallas kernels: 103 us -> 99.2 us
    pallas_call x1, Pallas kernels: 96.3 us -> 92.7 us  [fast_device(): pl.pallas_call(functools.partial(chain_kernel, cfg), out_shape=(pltpu.VME...]
where the time goes in v5:
time: 100 us
  Pallas kernels  99.2 us (99%)
    pallas_call x1, Pallas kernels, fast_device(): pl.pallas_call(functools.partial(chain_kernel, cfg), out_shape=(pltpu.VME...  92.7 us
    pallas_call x1, Pallas kernels, fast_device(): pl.pallas_call(functools.partial(finish_kernel, (chunks, ready)), out_sha...  6.51 us

profile of v5, /device:TPU:0, one launch (start us, length us, event | category | flops | bytes accessed | tf_op | source)
XLA Modules:
  0.0 100.0 jit_solution(6737930563648244907)
XLA Ops:
  0.6 92.7 %chain.1 = (bf16[1,1024,4096]{2,1,0:T(8,128)(2,1)S(1)}, bf16[1,4096,1024]{2,1,0:T(8,128)(2,1)S(1)}, bf16[3,256,4096]{2,1,0:T(8,128)(2,1)S(1)}, bf16[3,256,1024]{...) custom-call(s32[1,3]{1,0:T(1,128)} %index_hbm.1, s32[1,2,3]{2,1,0:T(2,128)} %bitcast.1, bf16[1,4,32,1024]{3,2,1,0:T(8,128)(2,1)} %saved_hbm.1, ...), custom_call_target="tpu_custom_call" | custom-call | flops 32212254720 | bytes 16777216 | tf_op jit(solution)/shard_map/chain/pallas_call | solution.py:462
  93.3 6.5 %finish.1 = (bf16[1,1024,4096]{2,1,0:T(8,128)(2,1)}, bf16[1,4096,1024]{2,1,0:T(8,128)(2,1)}, bf16[1,3,32,1024]{3,2,1,0:T(8,128)(2,1)}) custom-call(bf16[1,1024,4096]{2,1,0:T(8,128)(2,1)S(1)} %get-tuple-element.8.gin_ref, bf16[1,4096,1024]{2,1,0:T(8,128)(2,1)S(1)} %get-tuple-element.9.gout_ref, bf16[3,256,4096]{2,1,0:T(8,128)(2,1)S(1)} %get-tuple-element.10.h, ...), custom_call_target="tpu_custom_call" | custom-call | flops 6442450944 | bytes 33554432 | tf_op jit(solution)/shard_map/finish/pallas_call | solution.py:507

commit v6 on v5

--- a/solution.py
+++ b/solution.py
@@ -311,10 +311,13 @@
 
     for t in range(end):
         partial_dx(t)
-        if t > 0:
+        if t == 0:
+            ag_forward(t + 1)
+        else:
             grams(t)
         squares(t)
-        ag_forward(t + 1)
+        if t > 0:
+            ag_forward(t + 1)
         over(0, count, lambda k: pair_sum(t, k))
 
         @pl.when(is_last)
@@ -429,11 +432,14 @@
     copies.append(pltpu.make_async_copy(res_ref, res_hbm, sem.at[2, 0]))
     for copy in copies:
         copy.start()
-    for i in range(ready, blocks):
-        at = pl.ds(i * span, span)
+    half = span // 2
+    pieces = [(i * span, span) for i in range(ready, blocks - 1)] + [((blocks - 1) * span, half), (blocks * span - half, half)]
+    for i, (start, size) in enumerate(pieces):
+        at = pl.ds(start, size)
+        to = pl.ds(start - ready * span, size)
         lhs = jnp.concatenate([h[t, :, at] for t in range(slots)], axis=0)
-        made[i - ready] = dot(lhs, dyc[...].reshape(slots * tokens, width), TN).astype(BF16)
-        copy = pltpu.make_async_copy(made.at[i - ready], gout_hbm.at[0, at], sem.at[1, i])
+        made[to] = dot(lhs, dyc[...].reshape(slots * tokens, width), TN).astype(BF16)
+        copy = pltpu.make_async_copy(made.at[to], gout_hbm.at[0, at], sem.at[1, ready + i])
         copy.start()
         copies.append(copy)
     for copy in copies:
@@ -513,7 +519,7 @@
         ),
         in_specs=[vmem] * 5,
         out_specs=[hbm] * 3,
-        scratch_shapes=[pltpu.VMEM((chunks - ready, local // chunks, width), BF16), dma((3, chunks))],
+        scratch_shapes=[pltpu.VMEM(((chunks - ready) * (local // chunks), width), BF16), dma((3, chunks + 1))],
         compiler_params=pltpu.CompilerParams(vmem_limit_bytes=8 * 1024 * 1024),
         cost_estimate=pl.CostEstimate(flops=2 * slots * tokens * width * local, bytes_accessed=8 * width * local, transcendentals=0),
         name="finish",

time: 100 us -> 99.7 us (level); the launches traced: 100 us -> 98.4 us
  Pallas kernels: 99.2 us -> 97.6 us
    pallas_call x1, Pallas kernels: 92.7 us -> 91.4 us  [fast_device(): pl.pallas_call(functools.partial(chain_kernel, cfg), out_shape=(pltpu.VME...]
where the time goes in v6:
time: 99.7 us; the launch traced here: 98.4 us
  Pallas kernels  97.6 us (98%)
    pallas_call x1, Pallas kernels, fast_device(): pl.pallas_call(functools.partial(chain_kernel, cfg), out_shape=(pltpu.VME...  91.4 us
    pallas_call x1, Pallas kernels, fast_device(): pl.pallas_call(functools.partial(finish_kernel, (chunks, ready)), out_sha...  6.19 us

profile of v6, /device:TPU:0, one launch (start us, length us, event | category | flops | bytes accessed | tf_op | source)
XLA Modules:
  0.0 98.4 jit_solution(8393920929815898902)
XLA Ops:
  0.6 91.4 %chain.1 = (bf16[1,1024,4096]{2,1,0:T(8,128)(2,1)S(1)}, bf16[1,4096,1024]{2,1,0:T(8,128)(2,1)S(1)}, bf16[3,256,4096]{2,1,0:T(8,128)(2,1)S(1)}, bf16[3,256,1024]{...) custom-call(s32[1,3]{1,0:T(1,128)} %index_hbm.1, s32[1,2,3]{2,1,0:T(2,128)} %bitcast.1, bf16[1,4,32,1024]{3,2,1,0:T(8,128)(2,1)} %saved_hbm.1, ...), custom_call_target="tpu_custom_call" | custom-call | flops 32212254720 | bytes 16777216 | tf_op jit(solution)/shard_map/chain/pallas_call | solution.py:468
  92.0 6.2 %finish.1 = (bf16[1,1024,4096]{2,1,0:T(8,128)(2,1)}, bf16[1,4096,1024]{2,1,0:T(8,128)(2,1)}, bf16[1,3,32,1024]{3,2,1,0:T(8,128)(2,1)}) custom-call(bf16[1,1024,4096]{2,1,0:T(8,128)(2,1)S(1)} %get-tuple-element.8.gin_ref, bf16[1,4096,1024]{2,1,0:T(8,128)(2,1)S(1)} %get-tuple-element.9.gout_ref, bf16[3,256,4096]{2,1,0:T(8,128)(2,1)S(1)} %get-tuple-element.10.h, ...), custom_call_target="tpu_custom_call" | custom-call | flops 6442450944 | bytes 33554432 | tf_op jit(solution)/shard_map/finish/pallas_call | solution.py:513
